TPU v7x, 32 devices: a whole 2x2x4 slice. The times are simulated.
32 devices in a mesh: ba: 4 (over x, core), ma: 4 (over z), row: 2 (over y).
Axes of the slice: x: 2, y: 2, z: 4, core: 2. Of those that a mesh axis runs over, the one named last changes fastest.
Arguments:
- tokens: bfloat16 [8, 256, 4096], P(('ba', 'row'), None, 'ma'), may hold values from -6 to 6
- attn_gain: bfloat16 [4096], P('ma'), may hold values from 0.25 to 1.75
- query_weight: bfloat16 [4096, 4096], P('row', 'ma'), may hold values from -0.046875 to 0.046875
- key_weight: bfloat16 [4096, 4096], P('row', 'ma'), may hold values from -0.046875 to 0.046875
- value_projection_matrix: bfloat16 [4096, 4096], P('row', 'ma'), may hold values from -0.09375 to 0.09375
- attention_output_matrix: bfloat16 [4096, 4096], P('ma', 'row'), may hold values from -0.125 to 0.125
- bucket_bias_matrix: float32 [32, 64], P(None, 'ma'), may hold values from -6 to 215, as said below
- ffn_gain: bfloat16 [4096], P('ma'), may hold values from 0.25 to 1.75
- gate_weight: bfloat16 [4096, 8192], P(None, ('ma', 'row')), may hold values from -0.09375 to 0.09375
- up_weight: bfloat16 [4096, 8192], P(None, ('ma', 'row')), may hold values from -0.09375 to 0.09375
- down_projection_weight: bfloat16 [8192, 4096], P(('ma', 'row')), may hold values from -0.09375 to 0.09375
Outputs:
- encoded: bfloat16 [8, 256, 4096], P(('ba', 'row'), None, 'ma')
Inputs may be any that keep to these rules, and one draw needn't show every extreme that they name: `bucket_bias_matrix`: entries of the relative position table.
All inputs are finite; a program needn't handle non-finite values.
Results may differ from a plain program's by a relative error of at most 0.017.
Values may be sent and summed in bfloat16 or wider, within the bound.
A program may use at most 128 MiB of HBM per device.

v0:
```python
import functools

import jax
import jax.numpy as jnp
from jax import lax
from jax.experimental import pallas as pl
from jax.experimental.pallas import tpu as pltpu
from jax.sharding import PartitionSpec as P

bucket_thresholds = (1, 2, 3, 4, 5, 6, 7, 8, 11, 16, 23, 32, 45, 64, 91, 128)
epsilon = 1e-06


def buckets(length):
    places = jnp.arange(length, dtype=jnp.int32)
    offset = places[None, :] - places[:, None]
    distance = jnp.abs(offset)
    backward = jnp.zeros_like(distance)
    for threshold in bucket_thresholds[:15]:
        backward = backward + (distance >= threshold).astype(jnp.int32)
    forward = jnp.full_like(distance, 15)
    for threshold in bucket_thresholds:
        forward = forward + (distance >= threshold).astype(jnp.int32)
    return jnp.where(offset > 0, forward, backward)


def rms_scale(values, gain):
    mean_square = jnp.mean(values * values, axis=-1, keepdims=True)
    return (values * lax.rsqrt(mean_square + epsilon) * gain.astype(jnp.float32)).astype(
        jnp.bfloat16
    )


MESH = pl.DeviceIdType.MESH


def greet(me, count, row):
    barrier = pltpu.get_barrier_semaphore()

    @pl.when(me > 0)
    def _():
        pl.semaphore_signal(barrier, inc=1, device_id={"ma": me - 1}, device_id_type=MESH)

    @pl.when(me < count - 1)
    def _():
        pl.semaphore_signal(barrier, inc=1, device_id={"ma": me + 1}, device_id_type=MESH)

    pl.semaphore_signal(barrier, inc=1, device_id={"row": 1 - row}, device_id_type=MESH)
    inner = jnp.logical_and(me > 0, me < count - 1)
    pl.semaphore_wait(barrier, jnp.where(inner, 3, 2))


def gather_kernel(count, cuts, halved, x_ref, out_ref, local_sem, send_sem, z_sem, y_sem):
    me = lax.axis_index("ma")
    row = lax.axis_index("row")
    length, width = x_ref.shape
    pieces = len(cuts) - 1
    greet(me, count, row)

    def leaves(block):
        return block // (count // 2) == 1 - row if halved else block >= 0

    def comes(block):
        return block // (count // 2) == row if halved else block >= 0

    def place(block, piece, which):
        return out_ref.at[
            pl.ds(pl.multiple_of(which * length + cuts[piece], 16), cuts[piece + 1] - cuts[piece]),
            pl.ds(pl.multiple_of(block * width, width), width),
        ]

    def copy(way, block, piece, src=None):
        here = place(block, piece, row)
        target = ({"ma": me + 1}, {"ma": me - 1}, {"row": 1 - row})[way]
        sem = y_sem if way == 2 else z_sem
        return pltpu.make_async_remote_copy(
            src_ref=here if src is None else src,
            dst_ref=here,
            send_sem=send_sem.at[way, block, piece],
            recv_sem=sem.at[block, piece],
            device_id=target,
            device_id_type=MESH,
        )

    def own(piece):
        return x_ref.at[pl.ds(cuts[piece], cuts[piece + 1] - cuts[piece]), :]

    for piece in range(pieces):

        @pl.when(me < count - 1)
        def _():
            copy(0, me, piece, own(piece)).start()

        @pl.when(me > 0)
        def _():
            copy(1, me, piece, own(piece)).start()

        @pl.when(leaves(me))
        def _():
            copy(2, me, piece, own(piece)).start()

    mine = pltpu.make_async_copy(
        x_ref,
        out_ref.at[
            pl.ds(pl.multiple_of(row * length, length), length),
            pl.ds(pl.multiple_of(me * width, width), width),
        ],
        local_sem,
    )
    mine.start()
    for step in range(1, count):
        for piece in range(pieces):

            @pl.when(me - step >= 0)
            def _():
                block = me - step
                copy(0, block, piece).wait_recv()

                @pl.when(me < count - 1)
                def _():
                    copy(0, block, piece).start()

                @pl.when(leaves(block))
                def _():
                    copy(2, block, piece).start()

            @pl.when(me + step < count)
            def _():
                block = me + step
                copy(1, block, piece).wait_recv()

                @pl.when(me > 0)
                def _():
                    copy(1, block, piece).start()

                @pl.when(leaves(block))
                def _():
                    copy(2, block, piece).start()

    mine.wait()
    for block in range(count):
        for piece in range(pieces):
            here = place(block, piece, 1 - row)
            arrival = pltpu.make_async_remote_copy(
                src_ref=here,
                dst_ref=here,
                send_sem=send_sem.at[2, block, piece],
                recv_sem=y_sem.at[block, piece],
                device_id={"row": 1 - row},
                device_id_type=MESH,
            )

            @pl.when(comes(jnp.int32(block)))
            def _():
                arrival.wait_recv()

            @pl.when(leaves(jnp.int32(block)))
            def _():
                copy(2, block, piece).wait_send()

            @pl.when(jnp.logical_and(me < count - 1, block <= me))
            def _():
                copy(0, block, piece).wait_send()

            @pl.when(jnp.logical_and(me > 0, block >= me))
            def _():
                copy(1, block, piece).wait_send()


def gather_all(values, count, cuts, halved, collective_id):
    length, width = values.shape
    pieces = len(cuts) - 1
    return pl.pallas_call(
        functools.partial(gather_kernel, count, cuts, halved),
        out_shape=jax.ShapeDtypeStruct((2 * length, count * width), values.dtype),
        in_specs=[pl.BlockSpec(memory_space=pltpu.VMEM)],
        out_specs=pl.BlockSpec(memory_space=pltpu.VMEM),
        scratch_shapes=[
            pltpu.SemaphoreType.DMA,
            pltpu.SemaphoreType.DMA((3, count, pieces)),
            pltpu.SemaphoreType.DMA((count, pieces)),
            pltpu.SemaphoreType.DMA((count, pieces)),
        ],
        compiler_params=pltpu.CompilerParams(collective_id=collective_id, has_side_effects=True),
    )(values)


def reduce_kernel(count, pieces, paired, left_ref, right_ref, out_ref, *scratch):
    if paired:
        sent, landed, y_send, y_recv = scratch[:4]
    total, left_in, right_in, right_out, left_out, r_send, r_recv, l_send, l_recv = scratch[-9:]
    me = lax.axis_index("ma")
    row = lax.axis_index("row")
    length, width = out_ref.shape
    step_rows = length // pieces
    greet(me, count, row)

    def y_copy(unit):
        return pltpu.make_async_remote_copy(
            src_ref=sent.at[unit],
            dst_ref=landed.at[unit],
            send_sem=y_send.at[unit],
            recv_sem=y_recv.at[unit],
            device_id={"row": 1 - row},
            device_id_type=MESH,
        )

    def r_copy(unit):
        return pltpu.make_async_remote_copy(
            src_ref=right_out.at[unit],
            dst_ref=left_in.at[unit],
            send_sem=r_send.at[unit],
            recv_sem=r_recv.at[unit],
            device_id={"ma": me + 1},
            device_id_type=MESH,
        )

    def l_copy(unit):
        return pltpu.make_async_remote_copy(
            src_ref=left_out.at[unit],
            dst_ref=right_in.at[unit],
            send_sem=l_send.at[unit],
            recv_sem=l_recv.at[unit],
            device_id={"ma": me - 1},
            device_id_type=MESH,
        )

    def product(which, block, piece):
        start = pl.multiple_of(which * length + piece * step_rows, step_rows)
        columns = pl.ds(pl.multiple_of(block * width, width), width)
        return jnp.dot(
            left_ref[pl.ds(start, step_rows), :],
            right_ref[:, columns],
            preferred_element_type=jnp.float32,
        )

    def ordered(body):
        def turn(index, carry):
            piece = index % pieces
            side = index // pieces
            step = count - 1 - side // 2
            rightward = side % 2 == 0
            block = jnp.where(rightward, me + step, me - step)
            inside = jnp.logical_and(block >= 0, block < count)

            @pl.when(jnp.logical_and(inside, jnp.logical_or(step > 0, rightward)))
            def _():
                body(block, piece, block * pieces + piece)

            return carry

        lax.fori_loop(0, 2 * count * pieces, turn, 0)

    def send_peer(block, piece, unit):
        sent[unit] = product(1 - row, block, piece).astype(jnp.bfloat16)
        y_copy(unit).start()

    if paired:
        ordered(send_peer)

    def pass_on(block, piece, unit):
        total[...] = product(row if paired else 0, block, piece)
        if paired:
            y_copy(unit).wait_recv()
            total[...] = total[...] + landed[unit].astype(jnp.float32)

        @pl.when(jnp.logical_and(block >= me, me > 0))
        def _():
            r_copy(unit).wait_recv()
            total[...] = total[...] + left_in[unit].astype(jnp.float32)

        @pl.when(jnp.logical_and(block <= me, me < count - 1))
        def _():
            l_copy(unit).wait_recv()
            total[...] = total[...] + right_in[unit].astype(jnp.float32)

        @pl.when(block > me)
        def _():
            right_out[unit] = total[...].astype(jnp.bfloat16)
            r_copy(unit).start()

        @pl.when(block < me)
        def _():
            left_out[unit] = total[...].astype(jnp.bfloat16)
            l_copy(unit).start()

        @pl.when(block == me)
        def _():
            out_ref[pl.ds(pl.multiple_of(piece * step_rows, step_rows), step_rows), :] = total[...]

    ordered(pass_on)

    def drain(unit, carry):
        block = unit // pieces
        if paired:
            y_copy(unit).wait_send()

        @pl.when(block > me)
        def _():
            r_copy(unit).wait_send()

        @pl.when(block < me)
        def _():
            l_copy(unit).wait_send()

        return carry

    lax.fori_loop(0, count * pieces, drain, 0)


def reduce_all(left, right, count, pieces, paired, collective_id):
    length = left.shape[0] // (2 if paired else 1)
    width = right.shape[1] // count
    units = count * pieces
    blocks = pltpu.VMEM((units, length // pieces, width), jnp.bfloat16)
    sems = pltpu.SemaphoreType.DMA((units,))
    return pl.pallas_call(
        functools.partial(reduce_kernel, count, pieces, paired),
        out_shape=jax.ShapeDtypeStruct((length, width), jnp.float32),
        in_specs=[pl.BlockSpec(memory_space=pltpu.VMEM)] * 2,
        out_specs=pl.BlockSpec(memory_space=pltpu.VMEM),
        scratch_shapes=([blocks, blocks, sems, sems] if paired else [])
        + [pltpu.VMEM((length // pieces, width), jnp.float32)]
        + [blocks] * 4
        + [sems] * 4,
        compiler_params=pltpu.CompilerParams(
            collective_id=collective_id, has_side_effects=True, vmem_limit_bytes=60 * 2**20
        ),
    )(left, right)


def on_device(
    tokens,
    attn_gain,
    query_weight,
    key_weight,
    value_projection_matrix,
    attention_output_matrix,
    bucket_bias_matrix,
    ffn_gain,
    gate_weight,
    up_weight,
    down_projection_weight,
):
    sequences, length, part_width = tokens.shape
    ma_count = lax.axis_size("ma")
    local_heads = bucket_bias_matrix.shape[1]
    inner_width = query_weight.shape[1]
    head_size = inner_width // local_heads
    slab_rows = sequences * length
    token_rows = tokens.reshape(slab_rows, part_width)
    token_float = token_rows.astype(jnp.float32)
    row_count = lax.axis_size("row")
    half = query_weight.shape[0]
    swap = [(i, i ^ 1) for i in range(row_count)]
    my_row = lax.axis_index("row")
    ba_count = lax.axis_size("ba")
    lane = lax.axis_index("ba") % 4
    piece_rows = attention_output_matrix.shape[0] // 4
    out_piece = lax.dynamic_slice_in_dim(attention_output_matrix, lane * piece_rows, piece_rows, 0)
    out_piece = lax.ppermute(out_piece, "row", swap)
    out_across = lax.ppermute(out_piece, "ba", [(i, i ^ 2) for i in range(ba_count)])
    core_swap = [(i, i ^ 1) for i in range(ba_count)]
    out_pieces = [out_piece, lax.ppermute(out_piece, "ba", core_swap), out_across]
    out_pieces.append(lax.ppermute(out_across, "ba", core_swap))
    gains = jnp.concatenate(
        [attn_gain.reshape(1, part_width), ffn_gain.reshape(1, part_width)]
        + [jnp.zeros((14, part_width), jnp.bfloat16)]
    )
    padded = slab_rows + gains.shape[0]
    gathered = gather_all(
        jnp.concatenate([token_rows, gains]), ma_count, (0, slab_rows // 2, padded), True, 3
    )
    whole = lax.dynamic_slice_in_dim(gathered, my_row * padded, padded, 0)
    ffn_gain_full = whole[slab_rows + 1]
    own_float = whole[:slab_rows].astype(jnp.float32)
    scale = lax.rsqrt(jnp.mean(own_float * own_float, axis=-1, keepdims=True) + epsilon)
    gain_half = lax.dynamic_slice_in_dim(whole[slab_rows], my_row * half, half, 0)

    def with_gain(rows):
        return (rows.astype(jnp.float32) * gain_half.astype(jnp.float32)).astype(jnp.bfloat16)

    mine = with_gain(lax.dynamic_slice(whole, (0, my_row * half), (slab_rows, half)))
    arrived = with_gain(
        lax.dynamic_slice(
            gathered, ((1 - my_row) * padded, my_row * half), (slab_rows, half)
        )
    )
    weights_qkv = (query_weight, key_weight, value_projection_matrix)
    outgoing = [
        jnp.dot(arrived, matrix, preferred_element_type=jnp.float32).astype(jnp.bfloat16)
        for matrix in weights_qkv
    ]
    incoming = [lax.ppermute(part, "row", swap) for part in outgoing]
    projected = [
        (jnp.dot(mine, matrix, preferred_element_type=jnp.float32) + part.astype(jnp.float32)) * scale
        for matrix, part in zip(weights_qkv, incoming)
    ]
    query_heads, key_heads, value_heads = [
        member.astype(jnp.bfloat16).reshape(sequences, length, local_heads, head_size)
        for member in projected
    ]
    bucket_grid = buckets(length)
    table_rows = jnp.arange(bucket_bias_matrix.shape[0], dtype=jnp.int32)
    bucket_indicator = (table_rows[:, None, None] == bucket_grid[None, :, :]).astype(jnp.float32)
    relative_position_scores = jnp.einsum(
        "dmy,du->umy", bucket_indicator, bucket_bias_matrix, precision=lax.Precision.HIGHEST
    )
    scores = (
        jnp.einsum("sqhd,skhd->shqk", query_heads, key_heads, preferred_element_type=jnp.float32)
        + relative_position_scores[None]
    )
    row_max = jnp.max(scores, axis=-1, keepdims=True)
    exponent = jnp.exp(scores - row_max)
    weights = (exponent / jnp.sum(exponent, axis=-1, keepdims=True)).astype(jnp.bfloat16)
    attended = jnp.einsum(
        "shqk,skhd->sqhd", weights, value_heads, preferred_element_type=jnp.float32
    )
    attended = attended.astype(jnp.bfloat16).reshape(slab_rows, inner_width)
    out_far = jnp.zeros_like(attention_output_matrix)
    for offset, member in enumerate(out_pieces):
        out_far = lax.dynamic_update_slice_in_dim(
            out_far, member, (lane ^ offset) * piece_rows, 0
        )
    out_full = jnp.where(
        my_row == 0,
        jnp.concatenate([attention_output_matrix, out_far], axis=1),
        jnp.concatenate([out_far, attention_output_matrix], axis=1),
    )
    attn_out = reduce_all(attended, out_full, ma_count, 2, False, 2)
    residual_stream = (token_float + attn_out).astype(jnp.bfloat16)
    residual_f = residual_stream.astype(jnp.float32)
    gate_full, up_full, down_full = (gate_weight, up_weight, down_projection_weight)
    group_rows = gather_all(
        residual_stream, ma_count, (0, slab_rows // 2, slab_rows), False, 0
    )
    ffn_in = rms_scale(group_rows.astype(jnp.float32), ffn_gain_full)
    gate_act = jnp.dot(ffn_in, gate_full, preferred_element_type=jnp.float32)
    up_act = jnp.dot(ffn_in, up_full, preferred_element_type=jnp.float32)
    hidden = (jax.nn.gelu(gate_act, approximate=True) * up_act).astype(jnp.bfloat16)
    ffn_out = reduce_all(hidden, down_full, ma_count, 2, True, 1)
    encoded = (residual_f + ffn_out).astype(jnp.bfloat16)
    return encoded.reshape(sequences, length, part_width)


def solution(mesh):
    in_specs = (
        P(("ba", "row"), None, "ma"),
        P("ma"),
        P("row", "ma"),
        P("row", "ma"),
        P("row", "ma"),
        P("ma", "row"),
        P(None, "ma"),
        P("ma"),
        P(None, ("ma", "row")),
        P(None, ("ma", "row")),
        P(("ma", "row"), None),
    )
    out_specs = P(("ba", "row"), None, "ma")
    return jax.shard_map(
        on_device, mesh=mesh, in_specs=in_specs, out_specs=out_specs, check_vma=False
    )
```

profile of v0, /device:TPU:0, one launch (start us, length us, event | category | flops | bytes accessed | tf_op | source)
XLA Modules:
  0.0 299.8 jit_solution(12059832093436537249)
XLA Ops:
  1.3 3.1 %collective-permute-start.3 = (bf16[256,2048]{1,0:T(8,128)(2,1)S(1)}, bf16[256,2048]{1,0:T(8,128)(2,1)S(1)}, u32[]{:S(2)}, u32[]{:S(2)}) collective-permute-start(bf16[256,2048]{1,0:T(8,128)(2,1)S(1)} %constant_dynamic-slice_fusion), channel_id=1, source_target_pairs={{0,1},{1,0},{2,3},{3,2},{4,5},{5,4},{6,7},{7,6},{8,9},{9,8},{10,11... | collective-permute-start | bytes 3145736 | tf_op jit(solution)/shard_map/ppermute | solution.py:361
  5.8 2.0 maximum_maximum_fusion.x_ref
  7.8 48.2 %shard_map.109 = bf16[544,4096]{1,0:T(8,128)(2,1)} custom-call(bf16[272,1024]{1,0:T(8,128)(2,1)} %maximum_maximum_fusion.x_ref), custom_call_target="tpu_custom_call" | custom-call | tf_op jit(solution)/shard_map/pallas_call | solution.py:173
  57.0 4.8 %convolution_convert_fusion.2 = bf16[256,1024]{1,0:T(8,128)(2,1)} fusion(bf16[2048,1024]{1,0:T(8,128)(2,1)} %param.15, bf16[544,4096]{1,0:T(8,128)(2,1)} %shard_map.109, s32[]{:T(128)S(6)} %select_n.55, s32[]{:T(128)S(6)} %select_n.53, f32[2048]{0:T(1024)S(1)} %bitcast.39), kind=kOutput, calls=%fused_computation.30 | convolution fusion | flops 1075576832 | bytes 5775368 | tf_op jit(solution)/shard_map/dot_general | solution.py:391
  61.9 2.5 collective-permute-start
  64.3 3.3 %convolution_convert_fusion = bf16[256,1024]{1,0:T(8,128)(2,1)} fusion(bf16[2048,1024]{1,0:T(8,128)(2,1)S(1)} %copy-done.8, bf16[544,4096]{1,0:T(8,128)(2,1)} %shard_map.109, s32[]{:T(128)S(6)} %select_n.55, s32[]{:T(128)S(6)} %select_n.53, f32[2048]{0:T(1024)S(1)} %bitcast.40), kind=kOutput, calls=%fused_computation.28 | convolution fusion | flops 1075576832 | bytes 5775368 | tf_op jit(solution)/shard_map/dot_general | solution.py:391
  67.8 3.3 %convolution_convert_fusion.1 = bf16[256,1024]{1,0:T(8,128)(2,1)} fusion(bf16[2048,1024]{1,0:T(8,128)(2,1)S(1)} %copy-done.9, bf16[544,4096]{1,0:T(8,128)(2,1)} %shard_map.109, s32[]{:T(128)S(6)} %select_n.55, s32[]{:T(128)S(6)} %select_n.53, f32[2048]{0:T(1024)S(1)} %bitcast.41), kind=kOutput, calls=%fused_computation.29 | convolution fusion | flops 1075576832 | bytes 5775368 | tf_op jit(solution)/shard_map/dot_general | solution.py:391
  71.2 1.9 collective-permute-start.1
  74.2 2.1 multiply_reduce_fusion
  76.3 4.3 %fusion.4 = f32[256,256,16]{1,2,0:T(8,128)} fusion(s32[256,256]{1,0:T(8,128)S(1)} %fusion.25, f32[32,16]{0,1:T(8,128)S(1)} %copy-done), kind=kOutput, calls=%fused_computation.8 | convolution fusion | flops 404750336 | bytes 4458496 | tf_op jit(solution)/shard_map/dmy,du->umy/dot_general | solution.py:406
  80.6 5.3 %copy.21 = f32[256,256,16]{0,1,2:T(8,128)} copy(f32[256,256,16]{1,2,0:T(8,128)} %fusion.4) | data formatting | bytes 8388608 | tf_op jit(solution)/shard_map/dmy,du->umy/dot_general | solution.py:406
  85.9 2.6 collective-permute-done.2
  88.6 4.8 %multiply_convert_fusion.2 = bf16[256,1024]{1,0:T(8,128)(2,1)} fusion(bf16[256,1024]{1,0:T(8,128)(2,1)S(1)} %collective-permute-done.2, bf16[2048,1024]{1,0:T(8,128)(2,1)} %param.14, f32[2048]{0:T(1024)S(1)} %bitcast.42, bf16[544,4096]{1,0:T(8,128)(2,1)} %shard_map.109, s32[]{:T(128)S(6)} %select_n.52, s32[]{:T(128)S(6)} %select_n.54, ...), kind=kOutput, calls=%fused_computation.34 | convolution fusion | flops 1076363264 | bytes 6300680 | tf_op jit(solution)/shard_map/dot_general | solution.py:396
  93.3 1.5 collective-permute-start.5
  94.8 2.7 collective-permute-done.1
  97.6 3.6 %multiply_convert_fusion.3 = bf16[256,1024]{1,0:T(8,128)(2,1)} fusion(bf16[256,1024]{1,0:T(8,128)(2,1)} %collective-permute-done.1, bf16[2048,1024]{1,0:T(8,128)(2,1)S(1)} %copy-done.10, f32[2048]{0:T(1024)S(1)} %bitcast.43, bf16[544,4096]{1,0:T(8,128)(2,1)} %shard_map.109, s32[]{:T(128)S(6)} %select_n.52, s32[]{:T(128)S(6)} %select_n.54, ...), kind=kOutput, calls=%fused_computation.35 | convolution fusion | flops 1076363264 | bytes 6300680 | tf_op jit(solution)/shard_map/dot_general | solution.py:396
  102.6 3.1 %bitcast_add_fusion = f32[16,256,256]{1,2,0:T(8,128)S(1)} fusion(f32[256,256,16]{0,1,2:T(8,128)} %copy.21, bf16[256,16,64]{0,2,1:T(8,128)(2,1)S(1)} %bitcast.33, bf16[256,16,64]{0,2,1:T(8,128)(2,1)S(1)} %bitcast.32), kind=kOutput, calls=%fused_computation.9 | convolution fusion | flops 135266304 | bytes 9437184 | tf_op jit(solution)/shard_map/sqhd,skhd->shqk/dot_general | solution.py:410
  106.1 4.7 %multiply_convert_fusion.4 = bf16[256,1024]{1,0:T(8,128)(2,1)} fusion(bf16[256,1024]{1,0:T(8,128)(2,1)} %collective-permute-done, bf16[2048,1024]{1,0:T(8,128)(2,1)S(1)} %copy-done.11, f32[2048]{0:T(1024)S(1)} %bitcast.44, bf16[544,4096]{1,0:T(8,128)(2,1)} %shard_map.109, s32[]{:T(128)S(6)} %select_n.52, s32[]{:T(128)S(6)} %select_n.54, ...), kind=kOutput, calls=%fused_computation.36 | convolution fusion | flops 1076363264 | bytes 6300680 | tf_op jit(solution)/shard_map/dot_general | solution.py:396
  110.8 3.3 %collective-permute-done.5 = bf16[256,2048]{1,0:T(8,128)(2,1)S(1)} collective-permute-done((bf16[256,2048]{1,0:T(8,128)(2,1)S(1)}, bf16[256,2048]{1,0:T(8,128)(2,1)S(1)}, u32[]{:S(2)}, u32[]{:S(2)}) %collective-permute-start.5) | collective-permute-done | bytes 1048608 | tf_op jit(solution)/shard_map/ppermute | solution.py:362
  114.9 2.1 copy.18
  117.0 5.5 %fusion.16 = bf16[16,64,256]{2,1,0:T(8,128)(2,1)} fusion(bf16[256,16,64]{0,2,1:T(8,128)(2,1)} %bitcast.35, f32[16,256]{1,0:T(8,128)S(1)} %fusion.46, f32[16,256,256]{1,2,0:T(8,128)} %copy-done.2), kind=kOutput, calls=%fused_computation.27 | convolution fusion | flops 137629952 | bytes 5259264 | tf_op jit(solution)/shard_map/shqk,skhd->sqhd/dot_general | solution.py:416
  122.4 2.0 copy.23.left_ref
  125.3 1.5 constant_dynamic-update-slice_fusion
  127.5 5.5 %maximum_select_fusion.right_ref = bf16[1024,4096]{1,0:T(8,128)(2,1)} fusion(bf16[1024,2048]{1,0:T(8,128)(2,1)S(1)} %constant_dynamic-update-slice_fusion, bf16[1024,2048]{1,0:T(8,128)(2,1)S(1)} %copy-done.4, pred[]{:T(512)S(6)} %eq.21), kind=kLoop, calls=%fused_computation.6 | loop fusion | flops 37748736 | bytes 16777216 | tf_op jit(solution)/shard_map/jit(_where)/select_n | solution.py:425
  133.1 44.8 %shard_map.110 = f32[256,1024]{1,0:T(8,128)} custom-call(bf16[256,1024]{1,0:T(8,128)(2,1)} %copy.23.left_ref, bf16[1024,4096]{1,0:T(8,128)(2,1)} %maximum_select_fusion.right_ref), custom_call_target="tpu_custom_call" | custom-call | tf_op jit(solution)/shard_map/pallas_call | solution.py:317
  177.9 2.2 add_convert_fusion.1.x_ref
  180.1 49.5 %shard_map.111 = bf16[512,4096]{1,0:T(8,128)(2,1)} custom-call(bf16[256,1024]{1,0:T(8,128)(2,1)} %add_convert_fusion.1.x_ref), custom_call_target="tpu_custom_call" | custom-call | tf_op jit(solution)/shard_map/pallas_call | solution.py:173
  229.6 3.2 %fusion.1 = f32[512]{0:T(512)S(1)} fusion(bf16[512,4096]{1,0:T(8,128)(2,1)} %shard_map.111), kind=kLoop, calls=%fused_computation.3 | loop fusion | flops 6290944 | bytes 4196352 | tf_op jit(solution)/shard_map/reduce_sum | solution.py:28
  233.0 7.2 %fusion.18 = f32[512,1024]{1,0:T(8,128)S(1)} fusion(bf16[4096,1024]{1,0:T(8,128)(2,1)} %param.19, bf16[512,4096]{1,0:T(8,128)(2,1)S(1)} %copy-done.3, f32[4096]{0:T(1024)S(1)} %bitcast.37, f32[512]{0:T(512)S(1)} %add_rsqrt_fusion), kind=kOutput, calls=%fused_computation.31 | convolution fusion | flops 4303355904 | bytes 14698496 | tf_op jit(solution)/shard_map/dot_general | solution.py:438
  240.3 6.0 %fusion.14.left_ref = bf16[512,1024]{1,0:T(8,128)(2,1)} fusion(f32[512,1024]{1,0:T(8,128)S(1)} %fusion.18, bf16[4096,1024]{1,0:T(8,128)(2,1)S(1)} %bitcast.46, bf16[512,4096]{1,0:T(8,128)(2,1)S(1)} %copy-done.3, f32[4096]{0:T(1024)S(1)} %bitcast.38, f32[512]{0:T(512)S(1)} %add_rsqrt_fusion), kind=kOutput, calls=%fused_computation.23 | convolution fusion | flops 4308598784 | bytes 15747072 | tf_op jit(solution)/shard_map/dot_general | solution.py:439
  246.3 51.3 %shard_map.112 = f32[256,1024]{1,0:T(8,128)} custom-call(bf16[512,1024]{1,0:T(8,128)(2,1)} %fusion.14.left_ref, bf16[1024,4096]{1,0:T(8,128)(2,1)} %right_ref.1), custom_call_target="tpu_custom_call" | custom-call | tf_op jit(solution)/shard_map/pallas_call | solution.py:317
  297.6 2.2 fusion.23
  (53 shorter events, 9.4 us)
Async XLA Ops:
  0.0 76.3 %copy-start = (f32[32,16]{0,1:T(8,128)S(1)}, f32[32,16]{0,1:T(8,128)}, u32[]{:S(2)}) copy-start(f32[32,16]{0,1:T(8,128)} %param.17) | copy-start | bytes 6148
  1.3 92.0 %collective-permute-start.3 = (bf16[256,2048]{1,0:T(8,128)(2,1)S(1)}, bf16[256,2048]{1,0:T(8,128)(2,1)S(1)}, u32[]{:S(2)}, u32[]{:S(2)}) collective-permute-start(bf16[256,2048]{1,0:T(8,128)(2,1)S(1)} %constant_dynamic-slice_fusion), channel_id=1, source_target_pairs={{0,1},{1,0},{2,3},{3,2},{4,5},{5,4},{6,7},{7,6},{8,9},{9,8},{10,11... | collective-permute-start | bytes 3145736 | tf_op jit(solution)/shard_map/ppermute | solution.py:361
  56.0 8.3 %copy-start.8 = (bf16[2048,1024]{1,0:T(8,128)(2,1)S(1)}, bf16[2048,1024]{1,0:T(8,128)(2,1)}, u32[]{:S(2)}) copy-start(bf16[2048,1024]{1,0:T(8,128)(2,1)} %param.14) | copy-start | bytes 12582916
  61.9 6.0 %copy-start.9 = (bf16[2048,1024]{1,0:T(8,128)(2,1)S(1)}, bf16[2048,1024]{1,0:T(8,128)(2,1)}, u32[]{:S(2)}) copy-start(bf16[2048,1024]{1,0:T(8,128)(2,1)} %param.13) | copy-start | bytes 12582916
  61.9 44.0 %collective-permute-start = (bf16[256,1024]{1,0:T(8,128)(2,1)}, bf16[256,1024]{1,0:T(8,128)(2,1)}, u32[]{:S(2)}, u32[]{:S(2)}) collective-permute-start(bf16[256,1024]{1,0:T(8,128)(2,1)} %convolution_convert_fusion.2), channel_id=1, source_target_pairs={{0,1},{1,0},{2,3},{3,2},{4,5},{5,4},{6,7},{7,6},{8,9},{9,8},{10,11... | collective-permute-start | bytes 1572872 | tf_op jit(solution)/shard_map/ppermute | solution.py:394
  67.7 20.9 %collective-permute-start.2 = (bf16[256,1024]{1,0:T(8,128)(2,1)}, bf16[256,1024]{1,0:T(8,128)(2,1)S(1)}, u32[]{:S(2)}, u32[]{:S(2)}) collective-permute-start(bf16[256,1024]{1,0:T(8,128)(2,1)} %convolution_convert_fusion), channel_id=1, source_target_pairs={{0,1},{1,0},{2,3},{3,2},{4,5},{5,4},{6,7},{7,6},{8,9},{9,8},{10,11... | collective-permute-start | bytes 1572872 | tf_op jit(solution)/shard_map/ppermute | solution.py:394
  71.2 26.4 %collective-permute-start.1 = (bf16[256,1024]{1,0:T(8,128)(2,1)}, bf16[256,1024]{1,0:T(8,128)(2,1)}, u32[]{:S(2)}, u32[]{:S(2)}) collective-permute-start(bf16[256,1024]{1,0:T(8,128)(2,1)} %convolution_convert_fusion.1), channel_id=1, source_target_pairs={{0,1},{1,0},{2,3},{3,2},{4,5},{5,4},{6,7},{7,6},{8,9},{9,8},{10,11... | collective-permute-start | bytes 1572872 | tf_op jit(solution)/shard_map/ppermute | solution.py:394
  85.9 11.7 %copy-start.10 = (bf16[2048,1024]{1,0:T(8,128)(2,1)S(1)}, bf16[2048,1024]{1,0:T(8,128)(2,1)}, u32[]{:S(2)}) copy-start(bf16[2048,1024]{1,0:T(8,128)(2,1)} %param.13) | copy-start | bytes 12582916
  93.3 7.8 %copy-start.7 = (bf16[256,1024]{1,0:T(8,128)(2,1)S(1)}, bf16[256,1024]{1,0:T(8,128)(2,1)}, u32[]{:S(2)}) copy-start(bf16[256,1024]{1,0:T(8,128)(2,1)} %multiply_convert_fusion.2) | copy-start | bytes 1572868
  93.3 20.8 %collective-permute-start.5 = (bf16[256,2048]{1,0:T(8,128)(2,1)S(1)}, bf16[256,2048]{1,0:T(8,128)(2,1)S(1)}, u32[]{:S(2)}, u32[]{:S(2)}) collective-permute-start(bf16[256,2048]{1,0:T(8,128)(2,1)S(1)} %collective-permute-done.3), channel_id=1, source_target_pairs={{0,16},{8,24},{16,0},{24,8},{1,17},{9,25},{17,1},{25,9},{2,18},{10... | collective-permute-start | bytes 3145736 | tf_op jit(solution)/shard_map/ppermute | solution.py:362
  102.6 3.5 %copy-start.11 = (bf16[2048,1024]{1,0:T(8,128)(2,1)S(1)}, bf16[2048,1024]{1,0:T(8,128)(2,1)}, u32[]{:S(2)}) copy-start(bf16[2048,1024]{1,0:T(8,128)(2,1)} %param.15) | copy-start | bytes 12582916
  105.7 8.4 %copy-start.2 = (f32[16,256,256]{1,2,0:T(8,128)}, f32[16,256,256]{1,2,0:T(8,128)S(1)}, u32[]{:S(2)}) copy-start(f32[16,256,256]{1,2,0:T(8,128)S(1)} %bitcast_add_fusion) | copy-start | bytes 12582916
  105.7 19.4 %collective-permute-start.4 = (bf16[256,2048]{1,0:T(8,128)(2,1)S(1)}, bf16[256,2048]{1,0:T(8,128)(2,1)S(1)}, u32[]{:S(2)}, u32[]{:S(2)}) collective-permute-start(bf16[256,2048]{1,0:T(8,128)(2,1)S(1)} %collective-permute-done.3), channel_id=1, source_target_pairs={{0,8},{8,0},{16,24},{24,16},{1,9},{9,1},{17,25},{25,17},{2,10},{10... | collective-permute-start | bytes 3145736 | tf_op jit(solution)/shard_map/ppermute | solution.py:364
  114.1 11.2 %collective-permute-start.6 = (bf16[256,2048]{1,0:T(8,128)(2,1)S(1)}, bf16[256,2048]{1,0:T(8,128)(2,1)}, u32[]{:S(2)}, u32[]{:S(2)}) collective-permute-start(bf16[256,2048]{1,0:T(8,128)(2,1)S(1)} %collective-permute-done.5), channel_id=1, source_target_pairs={{0,8},{8,0},{16,24},{24,16},{1,9},{9,1},{17,25},{25,17},{2,10},{10... | collective-permute-start | bytes 3145736 | tf_op jit(solution)/shard_map/ppermute | solution.py:365
  125.0 2.5 copy-start.4
  133.1 44.8 %copy-start.6 = (bf16[1,256,1024]{2,1,0:T(8,128)(2,1)S(1)}, bf16[1,256,1024]{2,1,0:T(8,128)(2,1)}, u32[]{:S(2)}) copy-start(bf16[1,256,1024]{2,1,0:T(8,128)(2,1)} %param.11) | copy-start | bytes 1572868
  229.6 3.5 %copy-start.3 = (bf16[512,4096]{1,0:T(8,128)(2,1)S(1)}, bf16[512,4096]{1,0:T(8,128)(2,1)}, u32[]{:S(2)}) copy-start(bf16[512,4096]{1,0:T(8,128)(2,1)} %shard_map.111) | copy-start | bytes 12582916
  229.6 10.7 %slice-start = ((s8[8388608]{0:T(1024)(128)(4,1)}), s8[4194304]{0:T(1024)(128)(4,1)S(1)}, s32[]{:S(2)}) async-start(s8[8388608]{0:T(1024)(128)(4,1)} %bitcast.45), calls=%async_computation | async-start | bytes 8388608
  233.0 7.2 %slice-start.1 = ((s8[8388608]{0:T(1024)(128)(4,1)}), s8[4194304]{0:T(1024)(128)(4,1)S(1)}, s32[]{:S(2)}) async-start(s8[8388608]{0:T(1024)(128)(4,1)} %bitcast.45), calls=%async_computation.1 | async-start | bytes 8388608
  240.3 59.5 %copy-start.1 = (f32[32,16]{0,1:T(8,128)S(1)}, f32[32,16]{0,1:T(8,128)}, u32[]{:S(2)}) copy-start(f32[32,16]{0,1:T(8,128)} %param.17) | copy-start | bytes 6148
  246.3 51.3 %copy-start.5 = (bf16[256,1024]{1,0:T(8,128)(2,1)S(1)}, bf16[256,1024]{1,0:T(8,128)(2,1)}, u32[]{:S(2)}) copy-start(bf16[256,1024]{1,0:T(8,128)(2,1)} %add_convert_fusion.1.x_ref) | copy-start | bytes 1572868
where the time goes:
time: 301 us; the launch traced here: 300 us
  Pallas kernels  194 us (64%)
  matrix products  50.6 us (17%)
  other arithmetic  20.2 us (7%)
  local copies, waits for them, and re-layouts  17 us (6%)
  starting transfers between devices  9.12 us (3%)
  waiting for transfers between devices  8.74 us (3%)
    pallas_call x2, Pallas kernels, gather_all(): pl.pallas_call(functools.partial(gather_kernel, count, cuts, halved), out...  97.7 us
    pallas_call x2, Pallas kernels, reduce_all(): pl.pallas_call(functools.partial(reduce_kernel, count, pieces, paired), o...  96.1 us
    dot_general x3, matrix products, on_device(): jnp.dot(mine, matrix, preferred_element_type=jnp.float32)  13.1 us
    dot_general x3, matrix products, on_device(): jnp.dot(arrived, matrix, preferred_element_type=jnp.float32)  11.5 us
    dot_general x1, matrix products, on_device(): gate_act = jnp.dot(ffn_in, gate_full, preferred_element_type=jnp.float32)  7.22 us
  transfers between devices with their start and end apart: 7, of which 3 were waited for; matrix products, arithmetic and copies ran while one was open for 19% of the time, Pallas kernels for 16%

commit v1 on v0

--- a/solution.py
+++ b/solution.py
@@ -329,6 +329,534 @@
     )(left, right)
 
 
+def front_kernel(
+    count,
+    chunks,
+    groups,
+    tok_ref,
+    gain_ref,
+    table_ref,
+    wq_ref,
+    wk_ref,
+    wv_ref,
+    wo_ref,
+    att_ref,
+    gains_ref,
+    out_full_ref,
+    xs,
+    weights,
+    scaled,
+    part_out,
+    part_in,
+    sums_out,
+    sums_in,
+    bias,
+    gain_tile,
+    w_sem,
+    own_sem,
+    gain_sem,
+    wo_sem,
+    g_send,
+    g_recv,
+    y_send,
+    y_recv,
+    z_send,
+    z_recv,
+    p_send,
+    p_recv,
+    s_send,
+    s_recv,
+    wy_send,
+    wy_recv,
+    wf_send,
+    wf_recv,
+):
+    me = lax.axis_index("ma")
+    row = lax.axis_index("row")
+    ba = lax.axis_index("ba")
+    length, width = tok_ref.shape
+    half_blocks = count // 2
+    half = half_blocks * width
+    inner = att_ref.shape[1]
+    heads = table_ref.shape[1]
+    head_size = inner // heads
+    rows = length // chunks
+    group_width = inner // groups
+    home = me // half_blocks == row
+    col_half = wo_ref.shape[1]
+    pieces = wy_send.shape[0]
+    lane_rows = wo_ref.shape[0] // 4
+    piece_rows = lane_rows // pieces
+    lane = ba % 4
+
+    barrier = pltpu.get_barrier_semaphore()
+
+    def hello(offset, carry):
+        pl.semaphore_signal(
+            barrier, inc=1, device_id={"ma": (me + offset) % count}, device_id_type=MESH
+        )
+        return carry
+
+    lax.fori_loop(1, count, hello, 0)
+    pl.semaphore_signal(barrier, inc=1, device_id={"row": 1 - row}, device_id_type=MESH)
+    for flip in (1, 2, 3):
+        pl.semaphore_signal(barrier, inc=1, device_id={"ba": ba ^ flip}, device_id_type=MESH)
+    pl.semaphore_wait(barrier, count + 3)
+
+    def place(seq, chunk, slot):
+        return xs.at[
+            seq,
+            pl.ds(chunk * rows, rows),
+            pl.ds(pl.multiple_of(slot * width, width), width),
+        ]
+
+    def z_copy(way, seq, chunk, block, src=None):
+        slot = block - row * half_blocks
+        here = place(seq, chunk, slot)
+        return pltpu.make_async_remote_copy(
+            src_ref=here if src is None else src,
+            dst_ref=here,
+            send_sem=z_send.at[way, seq, chunk, slot],
+            recv_sem=z_recv.at[seq, chunk, slot],
+            device_id={"ma": me + 1 - 2 * way},
+            device_id_type=MESH,
+        )
+
+    def own(chunk):
+        return tok_ref.at[pl.ds(chunk * rows, rows), :]
+
+    def y_copy(chunk):
+        return pltpu.make_async_remote_copy(
+            src_ref=own(chunk),
+            dst_ref=place(row, chunk, me - (1 - row) * half_blocks),
+            send_sem=y_send.at[chunk],
+            recv_sem=y_recv.at[chunk],
+            device_id={"row": 1 - row},
+            device_id_type=MESH,
+        )
+
+    def y_arrival(chunk):
+        here = place(1 - row, chunk, me - row * half_blocks)
+        return pltpu.make_async_remote_copy(
+            src_ref=here,
+            dst_ref=here,
+            send_sem=y_send.at[chunk],
+            recv_sem=y_recv.at[chunk],
+            device_id={"row": 1 - row},
+            device_id_type=MESH,
+        )
+
+    def launch(mine, chunk):
+        seq = row if mine else 1 - row
+        src = own(chunk) if mine else None
+
+        @pl.when(home)
+        def _():
+            if not mine:
+                y_arrival(chunk).wait_recv()
+
+            @pl.when(me < count - 1)
+            def _():
+                z_copy(0, seq, chunk, me, src).start()
+
+            @pl.when(me > 0)
+            def _():
+                z_copy(1, seq, chunk, me, src).start()
+
+    def spread(mine, chunk):
+        seq = row if mine else 1 - row
+
+        def turn(step, carry):
+            for way in (0, 1):
+                block = me - step if way == 0 else me + step
+                inside = jnp.logical_and(
+                    block >= row * half_blocks, block < (row + 1) * half_blocks
+                )
+
+                @pl.when(inside)
+                def _():
+                    z_copy(way, seq, chunk, block).wait_recv()
+
+                    @pl.when(me < count - 1 if way == 0 else me > 0)
+                    def _():
+                        z_copy(way, seq, chunk, block).start()
+
+            return carry
+
+        lax.fori_loop(1, count, turn, 0)
+
+    def own_place():
+        return xs.at[
+            row, :, pl.ds(pl.multiple_of((me - row * half_blocks) * width, width), width)
+        ]
+
+    def gain_columns(block):
+        return gains_ref.at[:, pl.ds(pl.multiple_of(block * width, width), width)]
+
+    def gain_copy(offset):
+        return pltpu.make_async_remote_copy(
+            src_ref=gain_tile,
+            dst_ref=gain_columns(me),
+            send_sem=g_send.at[offset],
+            recv_sem=g_recv.at[me],
+            device_id={"ma": (me + offset) % count},
+            device_id_type=MESH,
+        )
+
+    def gain_arrival(block):
+        return pltpu.make_async_remote_copy(
+            src_ref=gain_tile,
+            dst_ref=gain_columns(block),
+            send_sem=g_send.at[0],
+            recv_sem=g_recv.at[block],
+            device_id={"ma": (me + 1) % count},
+            device_id_type=MESH,
+        )
+
+    def wo_region(owner, piece, side):
+        start = pl.multiple_of(owner * lane_rows + piece * piece_rows, piece_rows)
+        return out_full_ref.at[
+            pl.ds(start, piece_rows), pl.ds(pl.multiple_of(side * col_half, col_half), col_half)
+        ]
+
+    def wo_y(piece):
+        start = pl.multiple_of(lane * lane_rows + piece * piece_rows, piece_rows)
+        return pltpu.make_async_remote_copy(
+            src_ref=wo_ref.at[pl.ds(start, piece_rows), :],
+            dst_ref=wo_region(lane, piece, row),
+            send_sem=wy_send.at[piece],
+            recv_sem=wy_recv.at[piece],
+            device_id={"row": 1 - row},
+            device_id_type=MESH,
+        )
+
+    def wo_y_arrival(piece):
+        here = wo_region(lane, piece, 1 - row)
+        return pltpu.make_async_remote_copy(
+            src_ref=here,
+            dst_ref=here,
+            send_sem=wy_send.at[piece],
+            recv_sem=wy_recv.at[piece],
+            device_id={"row": 1 - row},
+            device_id_type=MESH,
+        )
+
+    def wo_fan(flip, piece, owner):
+        here = wo_region(owner, piece, 1 - row)
+        return pltpu.make_async_remote_copy(
+            src_ref=here,
+            dst_ref=here,
+            send_sem=wf_send.at[flip - 1, piece],
+            recv_sem=wf_recv.at[flip - 1, piece],
+            device_id={"ba": ba ^ flip},
+            device_id_type=MESH,
+        )
+
+    def part_copy(chunk, group):
+        return pltpu.make_async_remote_copy(
+            src_ref=part_out.at[chunk, group],
+            dst_ref=part_in.at[chunk, group],
+            send_sem=p_send.at[chunk, group],
+            recv_sem=p_recv.at[chunk, group],
+            device_id={"row": 1 - row},
+            device_id_type=MESH,
+        )
+
+    def sum_copy(chunk):
+        return pltpu.make_async_remote_copy(
+            src_ref=sums_out.at[chunk],
+            dst_ref=sums_in.at[chunk],
+            send_sem=s_send.at[chunk],
+            recv_sem=s_recv.at[chunk],
+            device_id={"row": 1 - row},
+            device_id_type=MESH,
+        )
+
+    launch(True, 0)
+
+    @pl.when(jnp.logical_not(home))
+    def _():
+        for chunk in range(chunks):
+            y_copy(chunk).start()
+
+    for piece in range(pieces):
+        wo_y(piece).start()
+
+    half_lines = lax.broadcasted_iota(jnp.int32, gain_tile.shape, 0) < 8
+    gain_tile[...] = jnp.where(
+        half_lines,
+        gain_ref[0:1, :].astype(jnp.float32),
+        gain_ref[1:2, :].astype(jnp.float32),
+    ).astype(jnp.bfloat16)
+
+    def gain_send(offset, carry):
+        gain_copy(offset).start()
+        return carry
+
+    lax.fori_loop(1, count, gain_send, 0)
+    gain_local = pltpu.make_async_copy(gain_tile, gain_columns(me), gain_sem)
+    gain_local.start()
+    own_local = pltpu.make_async_copy(tok_ref, own_place(), own_sem)
+
+    @pl.when(home)
+    def _():
+        own_local.start()
+
+    wo_local = pltpu.make_async_copy(
+        wo_ref,
+        out_full_ref.at[:, pl.ds(pl.multiple_of(row * col_half, col_half), col_half)],
+        wo_sem,
+    )
+    loads = [
+        pltpu.make_async_copy(matrix, weights.at[index], w_sem.at[index])
+        for index, matrix in enumerate((wq_ref, wk_ref, wv_ref))
+    ]
+    for load in loads:
+        load.start()
+    wo_local.start()
+
+    span = 2 * length
+    offset = lax.broadcasted_iota(jnp.int32, (8, span), 1) - (length - 1)
+    distance = jnp.abs(offset)
+    backward = jnp.zeros_like(distance)
+    for threshold in bucket_thresholds[:15]:
+        backward = backward + (distance >= threshold).astype(jnp.int32)
+    forward = jnp.full_like(distance, 15)
+    for threshold in bucket_thresholds:
+        forward = forward + (distance >= threshold).astype(jnp.int32)
+    bucket = jnp.where(offset > 0, forward, backward)
+
+    def build_bias(head, carry):
+        line = jnp.zeros((8, span), jnp.float32)
+        for entry in range(table_ref.shape[0]):
+            line = jnp.where(bucket == entry, table_ref[entry, head], line)
+        tile = jnp.broadcast_to(line[0:1, :], (length, span))
+        tile = pltpu.roll(tile, length + 1, 1, stride=1, stride_axis=0)
+        bias[head] = tile[:, :length]
+        return carry
+
+    lax.fori_loop(0, heads, build_bias, 0)
+    gain_local.wait()
+
+    @pl.when(home)
+    def _():
+        own_local.wait()
+
+    def gain_wait(step, carry):
+        gain_arrival((me + step) % count).wait_recv()
+        return carry
+
+    lax.fori_loop(1, count, gain_wait, 0)
+    gain_half = gains_ref[
+        pl.ds(0, 8), pl.ds(pl.multiple_of(row * half, half), half)
+    ][0:1, :].astype(jnp.float32)
+
+    def multiply_gain(seq, start, size):
+        values = xs[seq, pl.ds(start, size), :].astype(jnp.float32)
+        scaled[pl.ds(start, size), :] = (values * gain_half).astype(jnp.bfloat16)
+        return jnp.sum(values * values, axis=1, keepdims=True)
+
+    def outgoing(chunk):
+        squares = multiply_gain(1 - row, chunk * rows, rows)
+        sums_out[chunk] = jnp.broadcast_to(squares, (rows, 128))
+        sum_copy(chunk).start()
+
+        def turn(group, carry):
+            columns = pl.ds(pl.multiple_of(group * group_width, group_width), group_width)
+            for index in range(3):
+                part_out[chunk, group, :, pl.ds(index * group_width, group_width)] = jnp.dot(
+                    scaled[pl.ds(chunk * rows, rows), :],
+                    weights[index, :, columns],
+                    preferred_element_type=jnp.float32,
+                ).astype(jnp.bfloat16)
+            part_copy(chunk, group).start()
+            return carry
+
+        lax.fori_loop(0, groups, turn, 0)
+
+    def fan(piece):
+        wo_y_arrival(piece).wait_recv()
+        for flip in (1, 2, 3):
+            wo_fan(flip, piece, lane).start()
+
+    spread(True, 0)
+    launch(False, 0)
+    fan(0)
+    spread(False, 0)
+    launch(False, 1)
+    for load in loads:
+        load.wait()
+    fan(1)
+    outgoing(0)
+    spread(False, 1)
+    launch(True, 1)
+    fan(2)
+    outgoing(1)
+    fan(3)
+    spread(True, 1)
+    own_squares = multiply_gain(row, 0, length)
+    for chunk in range(chunks):
+        sum_copy(chunk).wait_recv()
+    other_squares = sums_in[...].reshape(length, 128)[:, 0:1]
+    scale = lax.rsqrt((own_squares + other_squares) / (count * width) + epsilon)
+    pair = 128 // head_size
+    first_lanes = lax.broadcasted_iota(jnp.int32, (length, 128), 1)
+
+    def attend(group, carry):
+        columns = pl.ds(pl.multiple_of(group * group_width, group_width), group_width)
+        products = [
+            jnp.dot(scaled[...], weights[index, :, columns], preferred_element_type=jnp.float32)
+            for index in range(3)
+        ]
+        for chunk in range(chunks):
+            part_copy(chunk, group).wait_recv()
+        query, key, value = [
+            (
+                (
+                    product
+                    + part_in[:, group, :, pl.ds(index * group_width, group_width)]
+                    .astype(jnp.float32)
+                    .reshape(length, group_width)
+                )
+                * scale
+            ).astype(jnp.bfloat16)
+            for index, product in enumerate(products)
+        ]
+        for tile in range(group_width // 128):
+            cut = slice(tile * 128, (tile + 1) * 128)
+            query_pair, key_pair, value_pair = query[:, cut], key[:, cut], value[:, cut]
+            outcome = None
+            for member in range(pair):
+                mask = jnp.logical_and(
+                    first_lanes >= member * head_size, first_lanes < (member + 1) * head_size
+                )
+                scores = (
+                    lax.dot_general(
+                        jnp.where(mask, query_pair.astype(jnp.float32), 0.0).astype(jnp.bfloat16),
+                        key_pair,
+                        (((1,), (1,)), ((), ())),
+                        preferred_element_type=jnp.float32,
+                    )
+                    + bias[group * (group_width // head_size) + tile * pair + member]
+                )
+                exponent = jnp.exp(scores - jnp.max(scores, axis=1, keepdims=True))
+                total = jnp.sum(exponent, axis=1, keepdims=True)
+                mixed = jnp.dot(
+                    (exponent / total).astype(jnp.bfloat16),
+                    value_pair,
+                    preferred_element_type=jnp.float32,
+                )
+                outcome = mixed if outcome is None else jnp.where(mask, mixed, outcome)
+            att_ref[
+                :, pl.ds(pl.multiple_of(group * group_width + tile * 128, 128), 128)
+            ] = outcome.astype(jnp.bfloat16)
+        return carry
+
+    lax.fori_loop(0, groups, attend, 0)
+
+    wo_local.wait()
+    for piece in range(pieces):
+        for flip in (1, 2, 3):
+            wo_fan(flip, piece, lane ^ flip).wait_recv()
+    for piece in range(pieces):
+        wo_y(piece).wait_send()
+        for flip in (1, 2, 3):
+            wo_fan(flip, piece, lane).wait_send()
+    for chunk in range(chunks):
+        sum_copy(chunk).wait_send()
+
+        def part_drain(group, carry):
+            part_copy(chunk, group).wait_send()
+            return carry
+
+        lax.fori_loop(0, groups, part_drain, 0)
+
+        @pl.when(jnp.logical_not(home))
+        def _():
+            y_copy(chunk).wait_send()
+
+        def z_drain(slot, carry):
+            block = slot + row * half_blocks
+            for seq in (0, 1):
+
+                @pl.when(jnp.logical_and(me < count - 1, block <= me))
+                def _():
+                    z_copy(0, seq, chunk, block).wait_send()
+
+                @pl.when(jnp.logical_and(me > 0, block >= me))
+                def _():
+                    z_copy(1, seq, chunk, block).wait_send()
+
+            return carry
+
+        lax.fori_loop(0, half_blocks, z_drain, 0)
+
+    def gain_drain(offset, carry):
+        gain_copy(offset).wait_send()
+        return carry
+
+    lax.fori_loop(1, count, gain_drain, 0)
+
+
+def front(tok, gains, table, wq, wk, wv, wo, count, collective_id):
+    length, width = tok.shape
+    chunks, pieces = 2, 4
+    inner = wq.shape[1]
+    heads = table.shape[1]
+    head_size = inner // heads
+    groups = max(1, inner // 256)
+    half = wq.shape[0]
+    rows = length // chunks
+    group_width = inner // groups
+    dma = pltpu.SemaphoreType.DMA
+    vmem = pl.BlockSpec(memory_space=pltpu.VMEM)
+    anywhere = pl.BlockSpec(memory_space=pl.ANY)
+    parts = pltpu.VMEM((chunks, groups, rows, 3 * group_width), jnp.bfloat16)
+    sums = pltpu.VMEM((chunks, rows, 128), jnp.float32)
+    return pl.pallas_call(
+        functools.partial(front_kernel, count, chunks, groups),
+        out_shape=(
+            jax.ShapeDtypeStruct((length, inner), jnp.bfloat16),
+            jax.ShapeDtypeStruct((16, count * width), jnp.bfloat16),
+            jax.ShapeDtypeStruct((wo.shape[0], 2 * wo.shape[1]), jnp.bfloat16),
+        ),
+        in_specs=[vmem, vmem, pl.BlockSpec(memory_space=pltpu.SMEM)] + [anywhere] * 4,
+        out_specs=(vmem, vmem, vmem),
+        scratch_shapes=[
+            pltpu.VMEM((2, length, half), jnp.bfloat16),
+            pltpu.VMEM((3, half, inner), jnp.bfloat16),
+            pltpu.VMEM((length, half), jnp.bfloat16),
+            parts,
+            parts,
+            sums,
+            sums,
+            pltpu.VMEM((heads, length, length), jnp.float32),
+            pltpu.VMEM((16, width), jnp.bfloat16),
+            dma((3,)),
+            dma,
+            dma,
+            dma,
+            dma((count,)),
+            dma((count,)),
+            dma((chunks,)),
+            dma((chunks,)),
+            dma((2, 2, chunks, count // 2)),
+            dma((2, chunks, count // 2)),
+            dma((chunks, groups)),
+            dma((chunks, groups)),
+            dma((chunks,)),
+            dma((chunks,)),
+            dma((pieces,)),
+            dma((pieces,)),
+            dma((3, pieces)),
+            dma((3, pieces)),
+        ],
+        compiler_params=pltpu.CompilerParams(
+            collective_id=collective_id, has_side_effects=True, vmem_limit_bytes=56 * 2**20
+        ),
+    )(tok, gains, table, wq, wk, wv, wo)
+
+
 def on_device(
     tokens,
     attn_gain,
@@ -344,89 +872,21 @@
 ):
     sequences, length, part_width = tokens.shape
     ma_count = lax.axis_size("ma")
-    local_heads = bucket_bias_matrix.shape[1]
-    inner_width = query_weight.shape[1]
-    head_size = inner_width // local_heads
     slab_rows = sequences * length
     token_rows = tokens.reshape(slab_rows, part_width)
     token_float = token_rows.astype(jnp.float32)
-    row_count = lax.axis_size("row")
-    half = query_weight.shape[0]
-    swap = [(i, i ^ 1) for i in range(row_count)]
-    my_row = lax.axis_index("row")
-    ba_count = lax.axis_size("ba")
-    lane = lax.axis_index("ba") % 4
-    piece_rows = attention_output_matrix.shape[0] // 4
-    out_piece = lax.dynamic_slice_in_dim(attention_output_matrix, lane * piece_rows, piece_rows, 0)
-    out_piece = lax.ppermute(out_piece, "row", swap)
-    out_across = lax.ppermute(out_piece, "ba", [(i, i ^ 2) for i in range(ba_count)])
-    core_swap = [(i, i ^ 1) for i in range(ba_count)]
-    out_pieces = [out_piece, lax.ppermute(out_piece, "ba", core_swap), out_across]
-    out_pieces.append(lax.ppermute(out_across, "ba", core_swap))
-    gains = jnp.concatenate(
-        [attn_gain.reshape(1, part_width), ffn_gain.reshape(1, part_width)]
-        + [jnp.zeros((14, part_width), jnp.bfloat16)]
+    attended, gains, out_full = front(
+        token_rows,
+        jnp.stack([attn_gain, ffn_gain]),
+        bucket_bias_matrix,
+        query_weight,
+        key_weight,
+        value_projection_matrix,
+        attention_output_matrix,
+        ma_count,
+        3,
     )
-    padded = slab_rows + gains.shape[0]
-    gathered = gather_all(
-        jnp.concatenate([token_rows, gains]), ma_count, (0, slab_rows // 2, padded), True, 3
-    )
-    whole = lax.dynamic_slice_in_dim(gathered, my_row * padded, padded, 0)
-    ffn_gain_full = whole[slab_rows + 1]
-    own_float = whole[:slab_rows].astype(jnp.float32)
-    scale = lax.rsqrt(jnp.mean(own_float * own_float, axis=-1, keepdims=True) + epsilon)
-    gain_half = lax.dynamic_slice_in_dim(whole[slab_rows], my_row * half, half, 0)
-
-    def with_gain(rows):
-        return (rows.astype(jnp.float32) * gain_half.astype(jnp.float32)).astype(jnp.bfloat16)
-
-    mine = with_gain(lax.dynamic_slice(whole, (0, my_row * half), (slab_rows, half)))
-    arrived = with_gain(
-        lax.dynamic_slice(
-            gathered, ((1 - my_row) * padded, my_row * half), (slab_rows, half)
-        )
-    )
-    weights_qkv = (query_weight, key_weight, value_projection_matrix)
-    outgoing = [
-        jnp.dot(arrived, matrix, preferred_element_type=jnp.float32).astype(jnp.bfloat16)
-        for matrix in weights_qkv
-    ]
-    incoming = [lax.ppermute(part, "row", swap) for part in outgoing]
-    projected = [
-        (jnp.dot(mine, matrix, preferred_element_type=jnp.float32) + part.astype(jnp.float32)) * scale
-        for matrix, part in zip(weights_qkv, incoming)
-    ]
-    query_heads, key_heads, value_heads = [
-        member.astype(jnp.bfloat16).reshape(sequences, length, local_heads, head_size)
-        for member in projected
-    ]
-    bucket_grid = buckets(length)
-    table_rows = jnp.arange(bucket_bias_matrix.shape[0], dtype=jnp.int32)
-    bucket_indicator = (table_rows[:, None, None] == bucket_grid[None, :, :]).astype(jnp.float32)
-    relative_position_scores = jnp.einsum(
-        "dmy,du->umy", bucket_indicator, bucket_bias_matrix, precision=lax.Precision.HIGHEST
-    )
-    scores = (
-        jnp.einsum("sqhd,skhd->shqk", query_heads, key_heads, preferred_element_type=jnp.float32)
-        + relative_position_scores[None]
-    )
-    row_max = jnp.max(scores, axis=-1, keepdims=True)
-    exponent = jnp.exp(scores - row_max)
-    weights = (exponent / jnp.sum(exponent, axis=-1, keepdims=True)).astype(jnp.bfloat16)
-    attended = jnp.einsum(
-        "shqk,skhd->sqhd", weights, value_heads, preferred_element_type=jnp.float32
-    )
-    attended = attended.astype(jnp.bfloat16).reshape(slab_rows, inner_width)
-    out_far = jnp.zeros_like(attention_output_matrix)
-    for offset, member in enumerate(out_pieces):
-        out_far = lax.dynamic_update_slice_in_dim(
-            out_far, member, (lane ^ offset) * piece_rows, 0
-        )
-    out_full = jnp.where(
-        my_row == 0,
-        jnp.concatenate([attention_output_matrix, out_far], axis=1),
-        jnp.concatenate([out_far, attention_output_matrix], axis=1),
-    )
+    ffn_gain_full = gains[8]
     attn_out = reduce_all(attended, out_full, ma_count, 2, False, 2)
     residual_stream = (token_float + attn_out).astype(jnp.bfloat16)
     residual_f = residual_stream.astype(jnp.float32)

time: 301 us -> 251 us (0.83)
  matrix products: 50.6 us -> 13.3 us
  Pallas kernels: 194 us -> 225 us
  local copies, waits for them, and re-layouts: 17 us -> 2.95 us
  other arithmetic: 20.2 us -> 9.03 us
  starting transfers between devices: 9.12 us -> 0 us
  waiting for transfers between devices: 8.74 us -> 0 us
    pallas_call x0 -> x1, Pallas kernels: none -> 86.1 us  [front(): pl.pallas_call(functools.partial(front_kernel, count, chunks, groups), ou...]
    pallas_call x2 -> x1, Pallas kernels: 97.7 us -> 47 us  [gather_all(): pl.pallas_call(functools.partial(gather_kernel, count, cuts, halved), out...]
    dot_general x9 -> x0, matrix products: 37.4 us -> none  [the longest x3 13.1 us: on_device(): jnp.dot(mine, matrix, preferred_element_type=jnp.float32)]
    ppermute x7 -> x0, starting transfers between devices: 9.12 us -> none  [the longest x3 4.51 us: on_device(): incoming = [lax.ppermute(part, 'row', swap) for part in outgoing]]
    ppermute x7 -> x0, waiting for transfers between devices: 8.74 us -> none  [the longest x3 5.39 us: on_device(): incoming = [lax.ppermute(part, 'row', swap) for part in outgoing]]
    select_n x2 -> x0, other arithmetic: 5.9 us -> none  [the longest x1 5.55 us: on_device(): jnp.where(my_row == 0, jnp.concatenate([attention_output_matrix, out_far]...]
    dot_general x1 -> x0, local copies, waits for them, and re-layouts: 5.28 us -> none  [on_device(): jnp.einsum('dmy,du->umy', bucket_indicator, bucket_bias_matrix, precision...]
    pallas_call x2, Pallas kernels: 96.1 us -> 91.6 us  [reduce_all(): pl.pallas_call(functools.partial(reduce_kernel, count, pieces, paired), o...]
  transfers between devices with their start and end apart: 7 -> 0, of which waited for: 3 -> 0; matrix products, arithmetic and copies ran while one was open for 19% -> 0% of each run, Pallas kernels for 16% -> 0%
where the time goes in v1:
time: 251 us; the launch traced here: 250 us
  Pallas kernels  225 us (90%)
  matrix products  13.3 us (5%)
  other arithmetic  9.03 us (4%)
  local copies, waits for them, and re-layouts  2.95 us (1%)
    pallas_call x2, Pallas kernels, reduce_all(): pl.pallas_call(functools.partial(reduce_kernel, count, pieces, paired), o...  91.6 us
    pallas_call x1, Pallas kernels, front(): pl.pallas_call(functools.partial(front_kernel, count, chunks, groups), ou...  86.1 us
    pallas_call x1, Pallas kernels, gather_all(): pl.pallas_call(functools.partial(gather_kernel, count, cuts, halved), out...  47 us
    dot_general x1, matrix products, on_device(): gate_act = jnp.dot(ffn_in, gate_full, preferred_element_type=jnp.float32)  7.23 us
    dot_general x1, matrix products, on_device(): up_act = jnp.dot(ffn_in, up_full, preferred_element_type=jnp.float32)  6.04 us

profile of v1, /device:TPU:0, one launch (start us, length us, event | category | flops | bytes accessed | tf_op | source)
XLA Modules:
  0.0 250.0 jit_solution(4244334686239204321)
XLA Ops:
  0.0 0.7 stack.9
  0.7 0.7 stack.10
  1.4 0.6 pad_maximum_fusion.gain_ref
  2.0 1.4 copy.12.table_ref
  3.4 86.1 %shard_map.109 = (bf16[256,1024]{1,0:T(8,128)(2,1)}, bf16[16,4096]{1,0:T(8,128)(2,1)}, bf16[1024,4096]{1,0:T(8,128)(2,1)}) custom-call(bf16[256,1024]{1,0:T(8,128)(2,1)} %bitcast.7, bf16[2,1024]{1,0:T(2,128)(2,1)} %pad_maximum_fusion.gain_ref, f32[32,16]{1,0:T(8,128)} %copy.12.table_ref, bf16[2048,1024]{1,0:T(8,128)(2,1)} %wq_ref.1, ...), custom_call_target="tpu_custom_call" | custom-call | tf_op jit(solution)/shard_map/pallas_call | solution.py:816
  89.4 0.0 copy-start.2
  89.4 40.3 %shard_map.110 = f32[256,1024]{1,0:T(8,128)} custom-call(bf16[256,1024]{1,0:T(8,128)(2,1)} %get-tuple-element.8.left_ref, bf16[1024,4096]{1,0:T(8,128)(2,1)} %get-tuple-element.9.right_ref), custom_call_target="tpu_custom_call" | custom-call | tf_op jit(solution)/shard_map/pallas_call | solution.py:317
  129.7 0.0 copy-done.2
  129.7 2.2 add_convert_fusion.1.x_ref
  131.9 0.8 slice_convert_fusion
  132.8 47.0 %shard_map.111 = bf16[512,4096]{1,0:T(8,128)(2,1)} custom-call(bf16[256,1024]{1,0:T(8,128)(2,1)} %add_convert_fusion.1.x_ref), custom_call_target="tpu_custom_call" | custom-call | tf_op jit(solution)/shard_map/pallas_call | solution.py:173
  179.7 0.0 copy-start
  179.7 0.0 slice-start
  179.8 3.2 %fusion = f32[512]{0:T(512)S(1)} fusion(bf16[512,4096]{1,0:T(8,128)(2,1)} %shard_map.111), kind=kLoop, calls=%fused_computation.2 | loop fusion | flops 6290944 | bytes 4196352 | tf_op jit(solution)/shard_map/reduce_sum | solution.py:28
  183.0 0.2 copy-done
  183.2 0.0 slice-start.1
  183.2 7.2 %fusion.13 = f32[512,1024]{1,0:T(8,128)S(1)} fusion(bf16[4096,1024]{1,0:T(8,128)(2,1)} %param.19, bf16[512,4096]{1,0:T(8,128)(2,1)S(1)} %copy-done, f32[4096]{0:T(1024)S(1)} %bitcast.8, f32[512]{0:T(512)S(1)} %add_rsqrt_fusion), kind=kOutput, calls=%fused_computation.15 | convolution fusion | flops 4303355904 | bytes 14698496 | tf_op jit(solution)/shard_map/dot_general | solution.py:898
  190.4 0.0 slice-done
  190.4 0.0 slice-done.1
  190.5 6.0 %fusion.11.left_ref = bf16[512,1024]{1,0:T(8,128)(2,1)} fusion(f32[512,1024]{1,0:T(8,128)S(1)} %fusion.13, bf16[4096,1024]{1,0:T(8,128)(2,1)S(1)} %bitcast.11, bf16[512,4096]{1,0:T(8,128)(2,1)S(1)} %copy-done, f32[4096]{0:T(1024)S(1)} %bitcast.9, f32[512]{0:T(512)S(1)} %add_rsqrt_fusion), kind=kOutput, calls=%fused_computation.14 | convolution fusion | flops 4308598784 | bytes 15747072 | tf_op jit(solution)/shard_map/dot_general | solution.py:899
  196.5 0.0 copy-start.1
  196.5 51.3 %shard_map.112 = f32[256,1024]{1,0:T(8,128)} custom-call(bf16[512,1024]{1,0:T(8,128)(2,1)} %fusion.11.left_ref, bf16[1024,4096]{1,0:T(8,128)(2,1)} %right_ref.1), custom_call_target="tpu_custom_call" | custom-call | tf_op jit(solution)/shard_map/pallas_call | solution.py:317
  247.8 0.0 copy-done.1
  247.9 2.2 fusion.15
  (2 shorter events, 0.0 us)
Async XLA Ops:
  89.4 40.3 %copy-start.2 = (bf16[1,256,1024]{2,1,0:T(8,128)(2,1)S(1)}, bf16[1,256,1024]{2,1,0:T(8,128)(2,1)}, u32[]{:S(2)}) copy-start(bf16[1,256,1024]{2,1,0:T(8,128)(2,1)} %param.11) | copy-start | bytes 1572868
  179.7 3.5 %copy-start = (bf16[512,4096]{1,0:T(8,128)(2,1)S(1)}, bf16[512,4096]{1,0:T(8,128)(2,1)}, u32[]{:S(2)}) copy-start(bf16[512,4096]{1,0:T(8,128)(2,1)} %shard_map.111) | copy-start | bytes 12582916
  179.7 10.7 %slice-start = ((s8[8388608]{0:T(1024)(128)(4,1)}), s8[4194304]{0:T(1024)(128)(4,1)S(1)}, s32[]{:S(2)}) async-start(s8[8388608]{0:T(1024)(128)(4,1)} %bitcast.10), calls=%async_computation | async-start | bytes 8388608
  183.2 7.3 %slice-start.1 = ((s8[8388608]{0:T(1024)(128)(4,1)}), s8[4194304]{0:T(1024)(128)(4,1)S(1)}, s32[]{:S(2)}) async-start(s8[8388608]{0:T(1024)(128)(4,1)} %bitcast.10), calls=%async_computation.1 | async-start | bytes 8388608
  196.5 51.4 %copy-start.1 = (bf16[256,1024]{1,0:T(8,128)(2,1)S(1)}, bf16[256,1024]{1,0:T(8,128)(2,1)}, u32[]{:S(2)}) copy-start(bf16[256,1024]{1,0:T(8,128)(2,1)} %add_convert_fusion.1.x_ref) | copy-start | bytes 1572868

commit v2 on v1

--- a/solution.py
+++ b/solution.py
@@ -11,26 +11,6 @@
 epsilon = 1e-06
 
 
-def buckets(length):
-    places = jnp.arange(length, dtype=jnp.int32)
-    offset = places[None, :] - places[:, None]
-    distance = jnp.abs(offset)
-    backward = jnp.zeros_like(distance)
-    for threshold in bucket_thresholds[:15]:
-        backward = backward + (distance >= threshold).astype(jnp.int32)
-    forward = jnp.full_like(distance, 15)
-    for threshold in bucket_thresholds:
-        forward = forward + (distance >= threshold).astype(jnp.int32)
-    return jnp.where(offset > 0, forward, backward)
-
-
-def rms_scale(values, gain):
-    mean_square = jnp.mean(values * values, axis=-1, keepdims=True)
-    return (values * lax.rsqrt(mean_square + epsilon) * gain.astype(jnp.float32)).astype(
-        jnp.bfloat16
-    )
-
-
 MESH = pl.DeviceIdType.MESH
 
 
@@ -48,285 +28,6 @@
     pl.semaphore_signal(barrier, inc=1, device_id={"row": 1 - row}, device_id_type=MESH)
     inner = jnp.logical_and(me > 0, me < count - 1)
     pl.semaphore_wait(barrier, jnp.where(inner, 3, 2))
-
-
-def gather_kernel(count, cuts, halved, x_ref, out_ref, local_sem, send_sem, z_sem, y_sem):
-    me = lax.axis_index("ma")
-    row = lax.axis_index("row")
-    length, width = x_ref.shape
-    pieces = len(cuts) - 1
-    greet(me, count, row)
-
-    def leaves(block):
-        return block // (count // 2) == 1 - row if halved else block >= 0
-
-    def comes(block):
-        return block // (count // 2) == row if halved else block >= 0
-
-    def place(block, piece, which):
-        return out_ref.at[
-            pl.ds(pl.multiple_of(which * length + cuts[piece], 16), cuts[piece + 1] - cuts[piece]),
-            pl.ds(pl.multiple_of(block * width, width), width),
-        ]
-
-    def copy(way, block, piece, src=None):
-        here = place(block, piece, row)
-        target = ({"ma": me + 1}, {"ma": me - 1}, {"row": 1 - row})[way]
-        sem = y_sem if way == 2 else z_sem
-        return pltpu.make_async_remote_copy(
-            src_ref=here if src is None else src,
-            dst_ref=here,
-            send_sem=send_sem.at[way, block, piece],
-            recv_sem=sem.at[block, piece],
-            device_id=target,
-            device_id_type=MESH,
-        )
-
-    def own(piece):
-        return x_ref.at[pl.ds(cuts[piece], cuts[piece + 1] - cuts[piece]), :]
-
-    for piece in range(pieces):
-
-        @pl.when(me < count - 1)
-        def _():
-            copy(0, me, piece, own(piece)).start()
-
-        @pl.when(me > 0)
-        def _():
-            copy(1, me, piece, own(piece)).start()
-
-        @pl.when(leaves(me))
-        def _():
-            copy(2, me, piece, own(piece)).start()
-
-    mine = pltpu.make_async_copy(
-        x_ref,
-        out_ref.at[
-            pl.ds(pl.multiple_of(row * length, length), length),
-            pl.ds(pl.multiple_of(me * width, width), width),
-        ],
-        local_sem,
-    )
-    mine.start()
-    for step in range(1, count):
-        for piece in range(pieces):
-
-            @pl.when(me - step >= 0)
-            def _():
-                block = me - step
-                copy(0, block, piece).wait_recv()
-
-                @pl.when(me < count - 1)
-                def _():
-                    copy(0, block, piece).start()
-
-                @pl.when(leaves(block))
-                def _():
-                    copy(2, block, piece).start()
-
-            @pl.when(me + step < count)
-            def _():
-                block = me + step
-                copy(1, block, piece).wait_recv()
-
-                @pl.when(me > 0)
-                def _():
-                    copy(1, block, piece).start()
-
-                @pl.when(leaves(block))
-                def _():
-                    copy(2, block, piece).start()
-
-    mine.wait()
-    for block in range(count):
-        for piece in range(pieces):
-            here = place(block, piece, 1 - row)
-            arrival = pltpu.make_async_remote_copy(
-                src_ref=here,
-                dst_ref=here,
-                send_sem=send_sem.at[2, block, piece],
-                recv_sem=y_sem.at[block, piece],
-                device_id={"row": 1 - row},
-                device_id_type=MESH,
-            )
-
-            @pl.when(comes(jnp.int32(block)))
-            def _():
-                arrival.wait_recv()
-
-            @pl.when(leaves(jnp.int32(block)))
-            def _():
-                copy(2, block, piece).wait_send()
-
-            @pl.when(jnp.logical_and(me < count - 1, block <= me))
-            def _():
-                copy(0, block, piece).wait_send()
-
-            @pl.when(jnp.logical_and(me > 0, block >= me))
-            def _():
-                copy(1, block, piece).wait_send()
-
-
-def gather_all(values, count, cuts, halved, collective_id):
-    length, width = values.shape
-    pieces = len(cuts) - 1
-    return pl.pallas_call(
-        functools.partial(gather_kernel, count, cuts, halved),
-        out_shape=jax.ShapeDtypeStruct((2 * length, count * width), values.dtype),
-        in_specs=[pl.BlockSpec(memory_space=pltpu.VMEM)],
-        out_specs=pl.BlockSpec(memory_space=pltpu.VMEM),
-        scratch_shapes=[
-            pltpu.SemaphoreType.DMA,
-            pltpu.SemaphoreType.DMA((3, count, pieces)),
-            pltpu.SemaphoreType.DMA((count, pieces)),
-            pltpu.SemaphoreType.DMA((count, pieces)),
-        ],
-        compiler_params=pltpu.CompilerParams(collective_id=collective_id, has_side_effects=True),
-    )(values)
-
-
-def reduce_kernel(count, pieces, paired, left_ref, right_ref, out_ref, *scratch):
-    if paired:
-        sent, landed, y_send, y_recv = scratch[:4]
-    total, left_in, right_in, right_out, left_out, r_send, r_recv, l_send, l_recv = scratch[-9:]
-    me = lax.axis_index("ma")
-    row = lax.axis_index("row")
-    length, width = out_ref.shape
-    step_rows = length // pieces
-    greet(me, count, row)
-
-    def y_copy(unit):
-        return pltpu.make_async_remote_copy(
-            src_ref=sent.at[unit],
-            dst_ref=landed.at[unit],
-            send_sem=y_send.at[unit],
-            recv_sem=y_recv.at[unit],
-            device_id={"row": 1 - row},
-            device_id_type=MESH,
-        )
-
-    def r_copy(unit):
-        return pltpu.make_async_remote_copy(
-            src_ref=right_out.at[unit],
-            dst_ref=left_in.at[unit],
-            send_sem=r_send.at[unit],
-            recv_sem=r_recv.at[unit],
-            device_id={"ma": me + 1},
-            device_id_type=MESH,
-        )
-
-    def l_copy(unit):
-        return pltpu.make_async_remote_copy(
-            src_ref=left_out.at[unit],
-            dst_ref=right_in.at[unit],
-            send_sem=l_send.at[unit],
-            recv_sem=l_recv.at[unit],
-            device_id={"ma": me - 1},
-            device_id_type=MESH,
-        )
-
-    def product(which, block, piece):
-        start = pl.multiple_of(which * length + piece * step_rows, step_rows)
-        columns = pl.ds(pl.multiple_of(block * width, width), width)
-        return jnp.dot(
-            left_ref[pl.ds(start, step_rows), :],
-            right_ref[:, columns],
-            preferred_element_type=jnp.float32,
-        )
-
-    def ordered(body):
-        def turn(index, carry):
-            piece = index % pieces
-            side = index // pieces
-            step = count - 1 - side // 2
-            rightward = side % 2 == 0
-            block = jnp.where(rightward, me + step, me - step)
-            inside = jnp.logical_and(block >= 0, block < count)
-
-            @pl.when(jnp.logical_and(inside, jnp.logical_or(step > 0, rightward)))
-            def _():
-                body(block, piece, block * pieces + piece)
-
-            return carry
-
-        lax.fori_loop(0, 2 * count * pieces, turn, 0)
-
-    def send_peer(block, piece, unit):
-        sent[unit] = product(1 - row, block, piece).astype(jnp.bfloat16)
-        y_copy(unit).start()
-
-    if paired:
-        ordered(send_peer)
-
-    def pass_on(block, piece, unit):
-        total[...] = product(row if paired else 0, block, piece)
-        if paired:
-            y_copy(unit).wait_recv()
-            total[...] = total[...] + landed[unit].astype(jnp.float32)
-
-        @pl.when(jnp.logical_and(block >= me, me > 0))
-        def _():
-            r_copy(unit).wait_recv()
-            total[...] = total[...] + left_in[unit].astype(jnp.float32)
-
-        @pl.when(jnp.logical_and(block <= me, me < count - 1))
-        def _():
-            l_copy(unit).wait_recv()
-            total[...] = total[...] + right_in[unit].astype(jnp.float32)
-
-        @pl.when(block > me)
-        def _():
-            right_out[unit] = total[...].astype(jnp.bfloat16)
-            r_copy(unit).start()
-
-        @pl.when(block < me)
-        def _():
-            left_out[unit] = total[...].astype(jnp.bfloat16)
-            l_copy(unit).start()
-
-        @pl.when(block == me)
-        def _():
-            out_ref[pl.ds(pl.multiple_of(piece * step_rows, step_rows), step_rows), :] = total[...]
-
-    ordered(pass_on)
-
-    def drain(unit, carry):
-        block = unit // pieces
-        if paired:
-            y_copy(unit).wait_send()
-
-        @pl.when(block > me)
-        def _():
-            r_copy(unit).wait_send()
-
-        @pl.when(block < me)
-        def _():
-            l_copy(unit).wait_send()
-
-        return carry
-
-    lax.fori_loop(0, count * pieces, drain, 0)
-
-
-def reduce_all(left, right, count, pieces, paired, collective_id):
-    length = left.shape[0] // (2 if paired else 1)
-    width = right.shape[1] // count
-    units = count * pieces
-    blocks = pltpu.VMEM((units, length // pieces, width), jnp.bfloat16)
-    sems = pltpu.SemaphoreType.DMA((units,))
-    return pl.pallas_call(
-        functools.partial(reduce_kernel, count, pieces, paired),
-        out_shape=jax.ShapeDtypeStruct((length, width), jnp.float32),
-        in_specs=[pl.BlockSpec(memory_space=pltpu.VMEM)] * 2,
-        out_specs=pl.BlockSpec(memory_space=pltpu.VMEM),
-        scratch_shapes=([blocks, blocks, sems, sems] if paired else [])
-        + [pltpu.VMEM((length // pieces, width), jnp.float32)]
-        + [blocks] * 4
-        + [sems] * 4,
-        compiler_params=pltpu.CompilerParams(
-            collective_id=collective_id, has_side_effects=True, vmem_limit_bytes=60 * 2**20
-        ),
-    )(left, right)
 
 
 def front_kernel(
@@ -340,8 +41,9 @@
     wk_ref,
     wv_ref,
     wo_ref,
+    share_ref,
+    gains_ref,
     att_ref,
-    gains_ref,
     out_full_ref,
     xs,
     weights,
@@ -758,6 +460,15 @@
     for piece in range(pieces):
         for flip in (1, 2, 3):
             wo_fan(flip, piece, lane ^ flip).wait_recv()
+
+    def project(block, carry):
+        columns = pl.ds(pl.multiple_of(block * width, width), width)
+        share_ref[block] = jnp.dot(
+            att_ref[...], out_full_ref[:, columns], preferred_element_type=jnp.float32
+        ).astype(jnp.bfloat16)
+        return carry
+
+    lax.fori_loop(0, count, project, 0)
     for piece in range(pieces):
         wo_y(piece).wait_send()
         for flip in (1, 2, 3):
@@ -816,13 +527,14 @@
     return pl.pallas_call(
         functools.partial(front_kernel, count, chunks, groups),
         out_shape=(
-            jax.ShapeDtypeStruct((length, inner), jnp.bfloat16),
+            jax.ShapeDtypeStruct((count, length, width), jnp.bfloat16),
             jax.ShapeDtypeStruct((16, count * width), jnp.bfloat16),
-            jax.ShapeDtypeStruct((wo.shape[0], 2 * wo.shape[1]), jnp.bfloat16),
         ),
         in_specs=[vmem, vmem, pl.BlockSpec(memory_space=pltpu.SMEM)] + [anywhere] * 4,
-        out_specs=(vmem, vmem, vmem),
+        out_specs=(vmem, vmem),
         scratch_shapes=[
+            pltpu.VMEM((length, inner), jnp.bfloat16),
+            pltpu.VMEM((wo.shape[0], 2 * wo.shape[1]), jnp.bfloat16),
             pltpu.VMEM((2, length, half), jnp.bfloat16),
             pltpu.VMEM((3, half, inner), jnp.bfloat16),
             pltpu.VMEM((length, half), jnp.bfloat16),
@@ -857,6 +569,376 @@
     )(tok, gains, table, wq, wk, wv, wo)
 
 
+def back_kernel(
+    count,
+    chunks,
+    share_ref,
+    gains_ref,
+    tok_ref,
+    gate_ref,
+    up_ref,
+    down_ref,
+    out_ref,
+    gate,
+    up,
+    down,
+    group,
+    normed,
+    hidden,
+    pair,
+    kept,
+    total,
+    c_out,
+    c_in,
+    e_out,
+    e_in,
+    y_out,
+    y_in,
+    w_sem,
+    c_send,
+    c_recv,
+    e_send,
+    e_recv,
+    y_send,
+    y_recv,
+    z_send,
+    z_recv,
+    x_send,
+    x_recv,
+):
+    me = lax.axis_index("ma")
+    row = lax.axis_index("row")
+    length, width = tok_ref.shape
+    rows = length // chunks
+    greet(me, count, row)
+
+    loads = [
+        pltpu.make_async_copy(source, target, w_sem.at[index])
+        for index, (source, target) in enumerate(
+            ((gate_ref, gate), (up_ref, up), (down_ref, down))
+        )
+    ]
+    for load in loads:
+        load.start()
+
+    def columns(block):
+        return pl.ds(pl.multiple_of(block * width, width), width)
+
+    def chunk_rows(chunk):
+        return pl.ds(pl.multiple_of(chunk * rows, rows), rows)
+
+    def hop(outs, ins, sends, recvs, chunk, block, rightward):
+        slot = block if rightward else jnp.where(block == me - 1, count, block)
+        return pltpu.make_async_remote_copy(
+            src_ref=outs.at[chunk, block],
+            dst_ref=ins.at[chunk, slot],
+            send_sem=sends.at[chunk, block],
+            recv_sem=recvs.at[chunk, slot],
+            device_id={"ma": me + 1 if rightward else me - 1},
+            device_id_type=MESH,
+        )
+
+    def landed(outs, ins, sends, recvs, chunk, slot, from_left):
+        return pltpu.make_async_remote_copy(
+            src_ref=outs.at[chunk, 0],
+            dst_ref=ins.at[chunk, slot],
+            send_sem=sends.at[chunk, 0],
+            recv_sem=recvs.at[chunk, slot],
+            device_id={"ma": me - 1 if from_left else me + 1},
+            device_id_type=MESH,
+        )
+
+    def across(chunk, block):
+        return pltpu.make_async_remote_copy(
+            src_ref=y_out.at[chunk, block],
+            dst_ref=y_in.at[chunk, block],
+            send_sem=y_send.at[chunk, block],
+            recv_sem=y_recv.at[chunk, block],
+            device_id={"row": 1 - row},
+            device_id_type=MESH,
+        )
+
+    def spot(chunk, seq, block):
+        return group.at[chunk, seq, :, columns(block)]
+
+    def pass_on(way, chunk, block):
+        here = spot(chunk, row, block)
+        return pltpu.make_async_remote_copy(
+            src_ref=here,
+            dst_ref=here,
+            send_sem=z_send.at[way, chunk, block],
+            recv_sem=z_recv.at[chunk, block],
+            device_id={"ma": me + 1 - 2 * way},
+            device_id_type=MESH,
+        )
+
+    def cross(chunk, seq, block):
+        here = spot(chunk, seq, block)
+        return pltpu.make_async_remote_copy(
+            src_ref=here,
+            dst_ref=here,
+            send_sem=x_send.at[chunk, block],
+            recv_sem=x_recv.at[chunk, block],
+            device_id={"row": 1 - row},
+            device_id_type=MESH,
+        )
+
+    def residual(chunk):
+        group[chunk, row, :, columns(me)] = (
+            tok_ref[chunk_rows(chunk), :].astype(jnp.float32) + total[...]
+        ).astype(jnp.bfloat16)
+        cross(chunk, row, me).start()
+
+        @pl.when(me < count - 1)
+        def _():
+            pass_on(0, chunk, me).start()
+
+        @pl.when(me > 0)
+        def _():
+            pass_on(1, chunk, me).start()
+
+    def encode(chunk):
+        out_ref[chunk_rows(chunk), :] = (
+            group[chunk, row, :, columns(me)].astype(jnp.float32) + total[...]
+        ).astype(jnp.bfloat16)
+
+    attention_line = (c_out, c_in, c_send, c_recv)
+    hidden_line = (e_out, e_in, e_send, e_recv)
+
+    def chain(line, chunk, step, last):
+        outs, ins, sends, recvs = line
+        for rightward in (True, False):
+            block = me + step if rightward else me - step
+            inside = jnp.logical_and(block >= 0, block < count)
+            if not rightward:
+                inside = jnp.logical_and(inside, step > 0)
+
+            @pl.when(inside)
+            def _():
+                if last:
+                    across(chunk, block).wait_recv()
+                    total[...] = kept[chunk, block] + y_in[chunk, block].astype(jnp.float32)
+                else:
+                    total[...] = share_ref[block, chunk_rows(chunk), :].astype(jnp.float32)
+
+                if rightward:
+
+                    @pl.when(me > 0)
+                    def _():
+                        landed(*line, chunk, block, True).wait_recv()
+                        total[...] = total[...] + ins[chunk, block].astype(jnp.float32)
+
+                    @pl.when(jnp.logical_and(step == 0, me < count - 1))
+                    def _():
+                        landed(*line, chunk, count, False).wait_recv()
+                        total[...] = total[...] + ins[chunk, count].astype(jnp.float32)
+
+                    @pl.when(step == 0)
+                    def _():
+                        if last:
+                            encode(chunk)
+                        else:
+                            residual(chunk)
+
+                    @pl.when(step > 0)
+                    def _():
+                        outs[chunk, block] = total[...].astype(jnp.bfloat16)
+                        hop(*line, chunk, block, True).start()
+
+                else:
+
+                    @pl.when(me < count - 1)
+                    def _():
+                        landed(*line, chunk, block, False).wait_recv()
+                        total[...] = total[...] + ins[chunk, block].astype(jnp.float32)
+
+                    outs[chunk, block] = total[...].astype(jnp.bfloat16)
+                    hop(*line, chunk, block, False).start()
+
+    def spread(chunk, step):
+        for way in (0, 1):
+            block = me - step if way == 0 else me + step
+
+            @pl.when(jnp.logical_and(block >= 0, block < count))
+            def _():
+                pass_on(way, chunk, block).wait_recv()
+                cross(chunk, row, block).start()
+
+                @pl.when(me < count - 1 if way == 0 else me > 0)
+                def _():
+                    pass_on(way, chunk, block).start()
+
+    tile = min(256, hidden.shape[1])
+    norm_rows = 16
+
+    def feed(chunk):
+        def arrive(block, carry):
+            cross(chunk, 1 - row, block).wait_recv()
+            return carry
+
+        lax.fori_loop(0, count, arrive, 0)
+        for seq in (0, 1):
+
+            def normalize(index, carry):
+                start = pl.multiple_of(index * norm_rows, norm_rows)
+                values = group[chunk, seq, pl.ds(start, norm_rows), :].astype(jnp.float32)
+                mean_square = jnp.mean(values * values, axis=1, keepdims=True)
+                normed[pl.ds(seq * rows + start, norm_rows), :] = (
+                    values
+                    * lax.rsqrt(mean_square + epsilon)
+                    * gains_ref[8:9, :].astype(jnp.float32)
+                ).astype(jnp.bfloat16)
+                return carry
+
+            lax.fori_loop(0, rows // norm_rows, normalize, 0)
+
+        @pl.when(chunk == 0)
+        def _():
+            for load in loads:
+                load.wait()
+
+        def gated(index, carry):
+            cut = pl.ds(pl.multiple_of(index * tile, tile), tile)
+            gate_act = jnp.dot(normed[...], gate[:, cut], preferred_element_type=jnp.float32)
+            up_act = jnp.dot(normed[...], up[:, cut], preferred_element_type=jnp.float32)
+            hidden[:, cut] = (jax.nn.gelu(gate_act, approximate=True) * up_act).astype(
+                jnp.bfloat16
+            )
+            return carry
+
+        lax.fori_loop(0, hidden.shape[1] // tile, gated, 0)
+
+        def contract(index, carry):
+            step = count - 1 - index // 2
+            rightward = index % 2 == 0
+            block = jnp.where(rightward, me + step, me - step)
+            inside = jnp.logical_and(block >= 0, block < count)
+
+            @pl.when(jnp.logical_and(inside, jnp.logical_or(step > 0, rightward)))
+            def _():
+                pair[...] = jnp.dot(
+                    hidden[...], down[:, columns(block)], preferred_element_type=jnp.float32
+                ).reshape(2, rows, width)
+                y_out[chunk, block] = pair[1 - row].astype(jnp.bfloat16)
+                across(chunk, block).start()
+                kept[chunk, block] = pair[row]
+
+            return carry
+
+        lax.fori_loop(0, 2 * count, contract, 0)
+
+    def tick(time, carry):
+        shifted = time + 4 * count
+        for line, base, last in (
+            (attention_line, 0, False),
+            (None, count - 1, False),
+            (hidden_line, 2 * count + 1, True),
+        ):
+            for index in reversed(range(count // 2)):
+                hop_index = 2 * index + (shifted - base) % 2
+                chunk = (shifted - base - hop_index) // 2 - 2 * count
+                active = jnp.logical_and(chunk >= 0, chunk < chunks)
+                if line is None:
+
+                    @pl.when(jnp.logical_and(active, hop_index > 0))
+                    def _():
+                        spread(chunk, hop_index)
+
+                else:
+
+                    @pl.when(active)
+                    def _():
+                        chain(line, chunk, count - 1 - hop_index, last)
+
+        chunk = shifted // 2 - 3 * count
+
+        @pl.when(
+            jnp.logical_and(time % 2 == 0, jnp.logical_and(chunk >= 0, chunk < chunks))
+        )
+        def _():
+            feed(chunk)
+
+        return carry
+
+    lax.fori_loop(0, 2 * chunks + 3 * count - 1, tick, 0)
+
+    def drain(index, carry):
+        chunk = index // count
+        block = index % count
+        across(chunk, block).wait_send()
+        cross(chunk, row, block).wait_send()
+
+        @pl.when(block > me)
+        def _():
+            hop(*attention_line, chunk, block, True).wait_send()
+            hop(*hidden_line, chunk, block, True).wait_send()
+
+        @pl.when(block < me)
+        def _():
+            hop(*attention_line, chunk, block, False).wait_send()
+            hop(*hidden_line, chunk, block, False).wait_send()
+
+        @pl.when(jnp.logical_and(me < count - 1, block <= me))
+        def _():
+            pass_on(0, chunk, block).wait_send()
+
+        @pl.when(jnp.logical_and(me > 0, block >= me))
+        def _():
+            pass_on(1, chunk, block).wait_send()
+
+        return carry
+
+    lax.fori_loop(0, chunks * count, drain, 0)
+
+
+def back(share, gains, tok, gate, up, down, count, chunks, collective_id):
+    length, width = tok.shape
+    rows = length // chunks
+    inner = down.shape[0]
+    dma = pltpu.SemaphoreType.DMA
+    vmem = pl.BlockSpec(memory_space=pltpu.VMEM)
+    anywhere = pl.BlockSpec(memory_space=pl.ANY)
+    line = pltpu.VMEM((chunks, count, rows, width), jnp.bfloat16)
+    longer = pltpu.VMEM((chunks, count + 1, rows, width), jnp.bfloat16)
+    return pl.pallas_call(
+        functools.partial(back_kernel, count, chunks),
+        out_shape=jax.ShapeDtypeStruct((length, width), jnp.bfloat16),
+        in_specs=[vmem, vmem, vmem] + [anywhere] * 3,
+        out_specs=vmem,
+        scratch_shapes=[
+            pltpu.VMEM(gate.shape, jnp.bfloat16),
+            pltpu.VMEM(up.shape, jnp.bfloat16),
+            pltpu.VMEM(down.shape, jnp.bfloat16),
+            pltpu.VMEM((chunks, 2, rows, count * width), jnp.bfloat16),
+            pltpu.VMEM((2 * rows, count * width), jnp.bfloat16),
+            pltpu.VMEM((2 * rows, inner), jnp.bfloat16),
+            pltpu.VMEM((2, rows, width), jnp.float32),
+            pltpu.VMEM((chunks, count, rows, width), jnp.float32),
+            pltpu.VMEM((rows, width), jnp.float32),
+            line,
+            longer,
+            line,
+            longer,
+            line,
+            line,
+            dma((3,)),
+            dma((chunks, count)),
+            dma((chunks, count + 1)),
+            dma((chunks, count)),
+            dma((chunks, count + 1)),
+            dma((chunks, count)),
+            dma((chunks, count)),
+            dma((2, chunks, count)),
+            dma((chunks, count)),
+            dma((chunks, count)),
+            dma((chunks, count)),
+        ],
+        compiler_params=pltpu.CompilerParams(
+            collective_id=collective_id, has_side_effects=True, vmem_limit_bytes=60 * 2**20
+        ),
+    )(share, gains, tok, gate, up, down)
+
+
 def on_device(
     tokens,
     attn_gain,
@@ -874,8 +956,7 @@
     ma_count = lax.axis_size("ma")
     slab_rows = sequences * length
     token_rows = tokens.reshape(slab_rows, part_width)
-    token_float = token_rows.astype(jnp.float32)
-    attended, gains, out_full = front(
+    share, gains = front(
         token_rows,
         jnp.stack([attn_gain, ffn_gain]),
         bucket_bias_matrix,
@@ -886,20 +967,17 @@
         ma_count,
         3,
     )
-    ffn_gain_full = gains[8]
-    attn_out = reduce_all(attended, out_full, ma_count, 2, False, 2)
-    residual_stream = (token_float + attn_out).astype(jnp.bfloat16)
-    residual_f = residual_stream.astype(jnp.float32)
-    gate_full, up_full, down_full = (gate_weight, up_weight, down_projection_weight)
-    group_rows = gather_all(
-        residual_stream, ma_count, (0, slab_rows // 2, slab_rows), False, 0
+    encoded = back(
+        share,
+        gains,
+        token_rows,
+        gate_weight,
+        up_weight,
+        down_projection_weight,
+        ma_count,
+        4,
+        1,
     )
-    ffn_in = rms_scale(group_rows.astype(jnp.float32), ffn_gain_full)
-    gate_act = jnp.dot(ffn_in, gate_full, preferred_element_type=jnp.float32)
-    up_act = jnp.dot(ffn_in, up_full, preferred_element_type=jnp.float32)
-    hidden = (jax.nn.gelu(gate_act, approximate=True) * up_act).astype(jnp.bfloat16)
-    ffn_out = reduce_all(hidden, down_full, ma_count, 2, True, 1)
-    encoded = (residual_f + ffn_out).astype(jnp.bfloat16)
     return encoded.reshape(sequences, length, part_width)
 
 

time: 251 us -> 217 us (0.86)
  Pallas kernels: 225 us -> 211 us
  matrix products: 13.3 us -> 0 us
  other arithmetic: 9.03 us -> 0.6 us
    pallas_call x3 -> x1, Pallas kernels: 139 us -> 124 us  [back(): pl.pallas_call(functools.partial(back_kernel, count, chunks), out_shape=j...]
    dot_general x2 -> x0, matrix products: 13.3 us -> none  [the longest x1 7.23 us: on_device(): gate_act = jnp.dot(ffn_in, gate_full, preferred_element_type=jnp.float32)]
    reduce_sum x1 -> x0, other arithmetic: 3.23 us -> none  [rms_scale(): mean_square = jnp.mean(values * values, axis=-1, keepdims=True)]
where the time goes in v2:
time: 217 us; the launch traced here: 216 us
  Pallas kernels  211 us (97%)
  local copies, waits for them, and re-layouts  4.61 us (2%)
    pallas_call x1, Pallas kernels, back(): pl.pallas_call(functools.partial(back_kernel, count, chunks), out_shape=j...  124 us
    pallas_call x1, Pallas kernels, front(): pl.pallas_call(functools.partial(front_kernel, count, chunks, groups), ou...  86.8 us

profile of v2, /device:TPU:0, one launch (start us, length us, event | category | flops | bytes accessed | tf_op | source)
XLA Modules:
  0.0 216.2 jit_solution(1276543488694172032)
XLA Ops:
  0.0 0.7 stack.9
  0.7 0.7 stack.10
  1.4 0.6 pad_maximum_fusion.gain_ref
  2.0 1.4 copy.12.table_ref
  3.4 86.8 %shard_map.109 = (bf16[4,256,1024]{2,1,0:T(8,128)(2,1)}, bf16[16,4096]{1,0:T(8,128)(2,1)}) custom-call(bf16[256,1024]{1,0:T(8,128)(2,1)} %bitcast.2, bf16[2,1024]{1,0:T(2,128)(2,1)} %pad_maximum_fusion.gain_ref, f32[32,16]{1,0:T(8,128)} %copy.12.table_ref, bf16[2048,1024]{1,0:T(8,128)(2,1)} %wq_ref.1, bf16[2048,1024]{1,0:T(8,128)(2,1)} %wk_ref.1, ...), custom_call_target="tpu_custom_call" | custom-call | tf_op jit(solution)/shard_map/pallas_call | solution.py:527
  90.2 124.1 %shard_map.110 = bf16[256,1024]{1,0:T(8,128)(2,1)} custom-call(bf16[4,256,1024]{2,1,0:T(8,128)(2,1)} %get-tuple-element.7.share_ref, bf16[16,4096]{1,0:T(8,128)(2,1)} %get-tuple-element.8.gains_ref, bf16[256,1024]{1,0:T(8,128)(2,1)} %bitcast.3, bf16[4096,1024]{1,0:T(8,128)(2,1)} %gate_ref.1, bf16[4096,1024]{1,0:T(8,128)(2,1)} %up_ref.1, ...), custom_call_target="tpu_custom_call" | custom-call | tf_op jit(solution)/shard_map/pallas_call | solution.py:903
  214.3 1.9 copy.14

commit v3 on v2

--- a/solution.py
+++ b/solution.py
@@ -35,7 +35,8 @@
     chunks,
     groups,
     tok_ref,
-    gain_ref,
+    attn_gain_ref,
+    ffn_gain_ref,
     table_ref,
     wq_ref,
     wk_ref,
@@ -53,6 +54,7 @@
     sums_out,
     sums_in,
     bias,
+    lines,
     gain_tile,
     w_sem,
     own_sem,
@@ -287,8 +289,8 @@
     half_lines = lax.broadcasted_iota(jnp.int32, gain_tile.shape, 0) < 8
     gain_tile[...] = jnp.where(
         half_lines,
-        gain_ref[0:1, :].astype(jnp.float32),
-        gain_ref[1:2, :].astype(jnp.float32),
+        jnp.broadcast_to(attn_gain_ref[...].astype(jnp.float32)[None, :], gain_tile.shape),
+        jnp.broadcast_to(ffn_gain_ref[...].astype(jnp.float32)[None, :], gain_tile.shape),
     ).astype(jnp.bfloat16)
 
     def gain_send(offset, carry):
@@ -328,11 +330,18 @@
         forward = forward + (distance >= threshold).astype(jnp.int32)
     bucket = jnp.where(offset > 0, forward, backward)
 
+    entries = lax.broadcasted_iota(jnp.int32, (table_ref.shape[0], span), 0)
+    chosen = (entries == jnp.broadcast_to(bucket[0:1, :], entries.shape)).astype(jnp.float32)
+    lines[...] = lax.dot_general(
+        table_ref[...],
+        chosen,
+        (((0,), (0,)), ((), ())),
+        precision=lax.Precision.HIGHEST,
+        preferred_element_type=jnp.float32,
+    )
+
     def build_bias(head, carry):
-        line = jnp.zeros((8, span), jnp.float32)
-        for entry in range(table_ref.shape[0]):
-            line = jnp.where(bucket == entry, table_ref[entry, head], line)
-        tile = jnp.broadcast_to(line[0:1, :], (length, span))
+        tile = jnp.broadcast_to(lines[pl.ds(head, 1), :], (length, span))
         tile = pltpu.roll(tile, length + 1, 1, stride=1, stride_axis=0)
         bias[head] = tile[:, :length]
         return carry
@@ -360,7 +369,10 @@
 
     def outgoing(chunk):
         squares = multiply_gain(1 - row, chunk * rows, rows)
-        sums_out[chunk] = jnp.broadcast_to(squares, (rows, 128))
+        for start in range(0, rows, 128):
+            sums_out[chunk, :, start : start + 128] = jnp.broadcast_to(
+                squares[start : start + 128], (128, 128)
+            ).T[0:8]
         sum_copy(chunk).start()
 
         def turn(group, carry):
@@ -399,7 +411,13 @@
     own_squares = multiply_gain(row, 0, length)
     for chunk in range(chunks):
         sum_copy(chunk).wait_recv()
-    other_squares = sums_in[...].reshape(length, 128)[:, 0:1]
+    other_squares = jnp.concatenate(
+        [
+            jnp.broadcast_to(sums_in[chunk, 0:1, start : start + 128], (128, 128)).T[:, 0:1]
+            for chunk in range(chunks)
+            for start in range(0, rows, 128)
+        ]
+    )
     scale = lax.rsqrt((own_squares + other_squares) / (count * width) + epsilon)
     pair = 128 // head_size
     first_lanes = lax.broadcasted_iota(jnp.int32, (length, 128), 1)
@@ -509,7 +527,7 @@
     lax.fori_loop(1, count, gain_drain, 0)
 
 
-def front(tok, gains, table, wq, wk, wv, wo, count, collective_id):
+def front(tok, attn_gain, ffn_gain, table, wq, wk, wv, wo, count, collective_id):
     length, width = tok.shape
     chunks, pieces = 2, 4
     inner = wq.shape[1]
@@ -523,14 +541,14 @@
     vmem = pl.BlockSpec(memory_space=pltpu.VMEM)
     anywhere = pl.BlockSpec(memory_space=pl.ANY)
     parts = pltpu.VMEM((chunks, groups, rows, 3 * group_width), jnp.bfloat16)
-    sums = pltpu.VMEM((chunks, rows, 128), jnp.float32)
+    sums = pltpu.VMEM((chunks, 8, rows), jnp.float32)
     return pl.pallas_call(
         functools.partial(front_kernel, count, chunks, groups),
         out_shape=(
             jax.ShapeDtypeStruct((count, length, width), jnp.bfloat16),
             jax.ShapeDtypeStruct((16, count * width), jnp.bfloat16),
         ),
-        in_specs=[vmem, vmem, pl.BlockSpec(memory_space=pltpu.SMEM)] + [anywhere] * 4,
+        in_specs=[vmem] * 4 + [anywhere] * 4,
         out_specs=(vmem, vmem),
         scratch_shapes=[
             pltpu.VMEM((length, inner), jnp.bfloat16),
@@ -543,6 +561,7 @@
             sums,
             sums,
             pltpu.VMEM((heads, length, length), jnp.float32),
+            pltpu.VMEM((heads, 2 * length), jnp.float32),
             pltpu.VMEM((16, width), jnp.bfloat16),
             dma((3,)),
             dma,
@@ -566,12 +585,14 @@
         compiler_params=pltpu.CompilerParams(
             collective_id=collective_id, has_side_effects=True, vmem_limit_bytes=56 * 2**20
         ),
-    )(tok, gains, table, wq, wk, wv, wo)
+    )(tok, attn_gain, ffn_gain, table, wq, wk, wv, wo)
 
 
 def back_kernel(
     count,
     chunks,
+    per,
+    spacing,
     share_ref,
     gains_ref,
     tok_ref,
@@ -605,6 +626,8 @@
     z_recv,
     x_send,
     x_recv,
+    r_send,
+    r_recv,
 ):
     me = lax.axis_index("ma")
     row = lax.axis_index("row")
@@ -682,6 +705,34 @@
             device_id={"row": 1 - row},
             device_id_type=MESH,
         )
+
+    middle = count // 2
+
+    def crosses(block):
+        return jnp.logical_not(
+            jnp.logical_or(
+                jnp.logical_and(block == 0, me >= middle),
+                jnp.logical_and(block == count - 1, me < middle),
+            )
+        )
+
+    def relay(end, chunk):
+        here = spot(chunk, 1 - row, end * (count - 1))
+        return pltpu.make_async_remote_copy(
+            src_ref=here,
+            dst_ref=here,
+            send_sem=r_send.at[end, chunk],
+            recv_sem=r_recv.at[end, chunk],
+            device_id={"ma": me + 1 - 2 * end},
+            device_id_type=MESH,
+        )
+
+    def relay_turn(end):
+        return me - (middle - 1) if end == 0 else middle - me
+
+    def relays(end):
+        turn = relay_turn(end)
+        return jnp.logical_and(turn >= 0, turn < middle)
 
     def residual(chunk):
         group[chunk, row, :, columns(me)] = (
@@ -762,7 +813,10 @@
             @pl.when(jnp.logical_and(block >= 0, block < count))
             def _():
                 pass_on(way, chunk, block).wait_recv()
-                cross(chunk, row, block).start()
+
+                @pl.when(crosses(block))
+                def _():
+                    cross(chunk, row, block).start()
 
                 @pl.when(me < count - 1 if way == 0 else me > 0)
                 def _():
@@ -771,28 +825,53 @@
     tile = min(256, hidden.shape[1])
     norm_rows = 16
 
-    def feed(chunk):
-        def arrive(block, carry):
-            cross(chunk, 1 - row, block).wait_recv()
+    def feed(batch):
+        def arrive(index, carry):
+            chunk = batch * per + index // count
+            block = index % count
+            first = block == 0
+            final = block == count - 1
+            taken = jnp.logical_or(
+                jnp.logical_and(first, relays(0)), jnp.logical_and(final, relays(1))
+            )
+
+            @pl.when(jnp.logical_and(crosses(block), jnp.logical_not(taken)))
+            def _():
+                cross(chunk, 1 - row, block).wait_recv()
+
+            for end in (0, 1):
+
+                @pl.when(
+                    jnp.logical_and(
+                        final if end else first,
+                        jnp.logical_not(jnp.logical_or(crosses(block), taken)),
+                    )
+                )
+                def _():
+                    relay(end, chunk).wait_recv()
+
             return carry
 
-        lax.fori_loop(0, count, arrive, 0)
-        for seq in (0, 1):
-
-            def normalize(index, carry):
-                start = pl.multiple_of(index * norm_rows, norm_rows)
-                values = group[chunk, seq, pl.ds(start, norm_rows), :].astype(jnp.float32)
-                mean_square = jnp.mean(values * values, axis=1, keepdims=True)
-                normed[pl.ds(seq * rows + start, norm_rows), :] = (
-                    values
-                    * lax.rsqrt(mean_square + epsilon)
-                    * gains_ref[8:9, :].astype(jnp.float32)
-                ).astype(jnp.bfloat16)
-                return carry
-
-            lax.fori_loop(0, rows // norm_rows, normalize, 0)
-
-        @pl.when(chunk == 0)
+        lax.fori_loop(0, per * count, arrive, 0)
+        strips = rows // norm_rows
+
+        def normalize(index, carry):
+            slab = index // strips
+            start = pl.multiple_of(index % strips * norm_rows, norm_rows)
+            values = group[
+                batch * per + slab // 2, slab % 2, pl.ds(start, norm_rows), :
+            ].astype(jnp.float32)
+            mean_square = jnp.mean(values * values, axis=1, keepdims=True)
+            normed[pl.ds(pl.multiple_of(index * norm_rows, norm_rows), norm_rows), :] = (
+                values
+                * lax.rsqrt(mean_square + epsilon)
+                * gains_ref[8:9, :].astype(jnp.float32)
+            ).astype(jnp.bfloat16)
+            return carry
+
+        lax.fori_loop(0, 2 * per * strips, normalize, 0)
+
+        @pl.when(batch == 0)
         def _():
             for load in loads:
                 load.wait()
@@ -818,55 +897,107 @@
             def _():
                 pair[...] = jnp.dot(
                     hidden[...], down[:, columns(block)], preferred_element_type=jnp.float32
-                ).reshape(2, rows, width)
-                y_out[chunk, block] = pair[1 - row].astype(jnp.bfloat16)
-                across(chunk, block).start()
-                kept[chunk, block] = pair[row]
+                ).reshape(per, 2, rows, width)
+                for sub in range(per):
+                    chunk = batch * per + sub
+                    y_out[chunk, block] = pair[sub, 1 - row].astype(jnp.bfloat16)
+                    across(chunk, block).start()
+                    kept[chunk, block] = pair[sub, row]
 
             return carry
 
         lax.fori_loop(0, 2 * count, contract, 0)
 
     def tick(time, carry):
-        shifted = time + 4 * count
-        for line, base, last in (
-            (attention_line, 0, False),
-            (None, count - 1, False),
-            (hidden_line, 2 * count + 1, True),
-        ):
-            for index in reversed(range(count // 2)):
-                hop_index = 2 * index + (shifted - base) % 2
-                chunk = (shifted - base - hop_index) // 2 - 2 * count
-                active = jnp.logical_and(chunk >= 0, chunk < chunks)
-                if line is None:
-
-                    @pl.when(jnp.logical_and(active, hop_index > 0))
+        def active(since):
+            return jnp.logical_and(
+                since % spacing == 0, jnp.logical_and(since >= 0, since < spacing * chunks)
+            )
+
+        def attention_turn(index, inner):
+            since = time - (count - 1) + index
+
+            @pl.when(active(since))
+            def _():
+                chain(attention_line, since // spacing, index, False)
+
+            return inner
+
+        def spread_turn(index, inner):
+            hop_index = count - 1 - index
+            since = time - (count - 1) - hop_index
+
+            @pl.when(active(since))
+            def _():
+                spread(since // spacing, hop_index)
+
+            return inner
+
+        def hidden_turn(index, inner):
+            since = time - hidden_base - (count - 1) + index
+
+            @pl.when(active(since))
+            def _():
+                chain(hidden_line, since // spacing, index, True)
+
+            return inner
+
+        def relay_all():
+            for end in (0, 1):
+                turn = relay_turn(end)
+                since = time - relay_base - turn
+                chunk = since // spacing
+
+                @pl.when(jnp.logical_and(relays(end), active(since)))
+                def _():
+                    @pl.when(turn == 0)
                     def _():
-                        spread(chunk, hop_index)
-
-                else:
-
-                    @pl.when(active)
+                        cross(chunk, 1 - row, end * (count - 1)).wait_recv()
+
+                    @pl.when(turn > 0)
                     def _():
-                        chain(line, chunk, count - 1 - hop_index, last)
-
-        chunk = shifted // 2 - 3 * count
-
-        @pl.when(
-            jnp.logical_and(time % 2 == 0, jnp.logical_and(chunk >= 0, chunk < chunks))
-        )
-        def _():
-            feed(chunk)
-
+                        relay(end, chunk).wait_recv()
+
+                    relay(end, chunk).start()
+
+        def feed_turn():
+            since = time - feed_base
+
+            @pl.when(
+                jnp.logical_and(
+                    since % (spacing * per) == 0,
+                    jnp.logical_and(since >= 0, since < spacing * chunks),
+                )
+            )
+            def _():
+                feed(since // (spacing * per))
+
+        lax.fori_loop(0, count - 1, spread_turn, 0)
+        lax.fori_loop(0, count, hidden_turn, 0)
+        lax.fori_loop(0, count, attention_turn, 0)
+        relay_all()
+        feed_turn()
         return carry
 
-    lax.fori_loop(0, 2 * chunks + 3 * count - 1, tick, 0)
+    feed_base = 2 * count
+    hidden_base = feed_base + 1
+    relay_base = 2 * count - middle
+    lax.fori_loop(0, spacing * (chunks - 1) + hidden_base + count, tick, 0)
 
     def drain(index, carry):
         chunk = index // count
         block = index % count
         across(chunk, block).wait_send()
-        cross(chunk, row, block).wait_send()
+
+        @pl.when(crosses(block))
+        def _():
+            cross(chunk, row, block).wait_send()
+
+        for end in (0, 1):
+
+            @pl.when(jnp.logical_and(block == end, relays(end)))
+            def _():
+                relay(end, chunk).wait_send()
 
         @pl.when(block > me)
         def _():
@@ -894,6 +1025,7 @@
 def back(share, gains, tok, gate, up, down, count, chunks, collective_id):
     length, width = tok.shape
     rows = length // chunks
+    per, spacing = 1, 2
     inner = down.shape[0]
     dma = pltpu.SemaphoreType.DMA
     vmem = pl.BlockSpec(memory_space=pltpu.VMEM)
@@ -901,7 +1033,7 @@
     line = pltpu.VMEM((chunks, count, rows, width), jnp.bfloat16)
     longer = pltpu.VMEM((chunks, count + 1, rows, width), jnp.bfloat16)
     return pl.pallas_call(
-        functools.partial(back_kernel, count, chunks),
+        functools.partial(back_kernel, count, chunks, per, spacing),
         out_shape=jax.ShapeDtypeStruct((length, width), jnp.bfloat16),
         in_specs=[vmem, vmem, vmem] + [anywhere] * 3,
         out_specs=vmem,
@@ -910,9 +1042,9 @@
             pltpu.VMEM(up.shape, jnp.bfloat16),
             pltpu.VMEM(down.shape, jnp.bfloat16),
             pltpu.VMEM((chunks, 2, rows, count * width), jnp.bfloat16),
-            pltpu.VMEM((2 * rows, count * width), jnp.bfloat16),
-            pltpu.VMEM((2 * rows, inner), jnp.bfloat16),
-            pltpu.VMEM((2, rows, width), jnp.float32),
+            pltpu.VMEM((2 * per * rows, count * width), jnp.bfloat16),
+            pltpu.VMEM((2 * per * rows, inner), jnp.bfloat16),
+            pltpu.VMEM((per, 2, rows, width), jnp.float32),
             pltpu.VMEM((chunks, count, rows, width), jnp.float32),
             pltpu.VMEM((rows, width), jnp.float32),
             line,
@@ -932,6 +1064,8 @@
             dma((chunks, count)),
             dma((chunks, count)),
             dma((chunks, count)),
+            dma((2, chunks)),
+            dma((2, chunks)),
         ],
         compiler_params=pltpu.CompilerParams(
             collective_id=collective_id, has_side_effects=True, vmem_limit_bytes=60 * 2**20
@@ -958,7 +1092,8 @@
     token_rows = tokens.reshape(slab_rows, part_width)
     share, gains = front(
         token_rows,
-        jnp.stack([attn_gain, ffn_gain]),
+        attn_gain,
+        ffn_gain,
         bucket_bias_matrix,
         query_weight,
         key_weight,

time: 217 us -> 207 us (0.954)
  Pallas kernels: 211 us -> 203 us
    pallas_call x1, Pallas kernels: 124 us -> 119 us  [back(): pl.pallas_call(functools.partial(back_kernel, count, chunks, per, spacing...]
    pallas_call x1, Pallas kernels: 86.8 us -> 84.5 us  [front(): pl.pallas_call(functools.partial(front_kernel, count, chunks, groups), ou...]
where the time goes in v3:
time: 207 us; the launch traced here: 206 us
  Pallas kernels  203 us (98%)
  local copies, waits for them, and re-layouts  3.24 us (2%)
    pallas_call x1, Pallas kernels, back(): pl.pallas_call(functools.partial(back_kernel, count, chunks, per, spacing...  119 us
    pallas_call x1, Pallas kernels, front(): pl.pallas_call(functools.partial(front_kernel, count, chunks, groups), ou...  84.5 us

profile of v3, /device:TPU:0, one launch (start us, length us, event | category | flops | bytes accessed | tf_op | source)
XLA Modules:
  0.0 206.4 jit_solution(10260205504538146476)
XLA Ops:
  0.0 1.4 copy.12.table_ref
  1.4 84.5 %shard_map.109 = (bf16[4,256,1024]{2,1,0:T(8,128)(2,1)}, bf16[16,4096]{1,0:T(8,128)(2,1)}) custom-call(bf16[256,1024]{1,0:T(8,128)(2,1)} %bitcast.2, bf16[1024]{0:T(1024)(128)(2,1)} %attn_gain_ref.1, bf16[1024]{0:T(1024)(128)(2,1)} %ffn_gain_ref.1, f32[32,16]{1,0:T(8,128)} %copy.12.table_ref, bf16[2048,1024]{1,0:T(8,128)(2,1)} %wq_ref.1, ...), custom_call_target="tpu_custom_call" | custom-call | tf_op jit(solution)/shard_map/pallas_call | solution.py:545
  85.8 118.7 %shard_map.110 = bf16[256,1024]{1,0:T(8,128)(2,1)} custom-call(bf16[4,256,1024]{2,1,0:T(8,128)(2,1)} %get-tuple-element.7.share_ref, bf16[16,4096]{1,0:T(8,128)(2,1)} %get-tuple-element.8.gains_ref, bf16[256,1024]{1,0:T(8,128)(2,1)} %bitcast.3, bf16[4096,1024]{1,0:T(8,128)(2,1)} %gate_ref.1, bf16[4096,1024]{1,0:T(8,128)(2,1)} %up_ref.1, ...), custom_call_target="tpu_custom_call" | custom-call | tf_op jit(solution)/shard_map/pallas_call | solution.py:1035
  204.5 1.9 copy.14

commit v4 on v3

--- a/solution.py
+++ b/solution.py
@@ -14,26 +14,13 @@
 MESH = pl.DeviceIdType.MESH
 
 
-def greet(me, count, row):
-    barrier = pltpu.get_barrier_semaphore()
-
-    @pl.when(me > 0)
-    def _():
-        pl.semaphore_signal(barrier, inc=1, device_id={"ma": me - 1}, device_id_type=MESH)
-
-    @pl.when(me < count - 1)
-    def _():
-        pl.semaphore_signal(barrier, inc=1, device_id={"ma": me + 1}, device_id_type=MESH)
-
-    pl.semaphore_signal(barrier, inc=1, device_id={"row": 1 - row}, device_id_type=MESH)
-    inner = jnp.logical_and(me > 0, me < count - 1)
-    pl.semaphore_wait(barrier, jnp.where(inner, 3, 2))
-
-
-def front_kernel(
+def layer_kernel(
     count,
+    halves,
+    groups,
     chunks,
-    groups,
+    per,
+    spacing,
     tok_ref,
     attn_gain_ref,
     ffn_gain_ref,
@@ -42,21 +29,38 @@
     wk_ref,
     wv_ref,
     wo_ref,
-    share_ref,
-    gains_ref,
-    att_ref,
-    out_full_ref,
+    gate_ref,
+    up_ref,
+    down_ref,
+    out_ref,
+    qkv,
+    up,
+    out_full,
+    gains,
     xs,
-    weights,
     scaled,
     part_out,
     part_in,
     sums_out,
     sums_in,
-    bias,
     lines,
     gain_tile,
+    att,
+    share,
+    group,
+    normed,
+    hidden,
+    pair,
+    bias,
+    kept,
+    total,
+    c_out,
+    c_in,
+    e_in,
+    y_out,
+    y_in,
     w_sem,
+    d_sem,
     own_sem,
     gain_sem,
     wo_sem,
@@ -74,17 +78,33 @@
     wy_recv,
     wf_send,
     wf_recv,
+    c_send,
+    c_recv,
+    e_send,
+    e_recv,
+    a_send,
+    a_recv,
+    d_send,
+    d_recv,
+    x_send,
+    x_recv,
+    r_send,
+    r_recv,
 ):
+    rows = tok_ref.shape[0] // chunks
+    per_tile = bias.shape[3] // tok_ref.shape[0]
+    gate = qkv.at[pl.ds(0, gate_ref.shape[0]), :]
+    down = out_full
     me = lax.axis_index("ma")
     row = lax.axis_index("row")
     ba = lax.axis_index("ba")
     length, width = tok_ref.shape
     half_blocks = count // 2
     half = half_blocks * width
-    inner = att_ref.shape[1]
+    inner = qkv.shape[1]
     heads = table_ref.shape[1]
     head_size = inner // heads
-    rows = length // chunks
+    half_rows = length // halves
     group_width = inner // groups
     home = me // half_blocks == row
     col_half = wo_ref.shape[1]
@@ -110,7 +130,7 @@
     def place(seq, chunk, slot):
         return xs.at[
             seq,
-            pl.ds(chunk * rows, rows),
+            pl.ds(chunk * half_rows, half_rows),
             pl.ds(pl.multiple_of(slot * width, width), width),
         ]
 
@@ -127,7 +147,7 @@
         )
 
     def own(chunk):
-        return tok_ref.at[pl.ds(chunk * rows, rows), :]
+        return tok_ref.at[pl.ds(chunk * half_rows, half_rows), :]
 
     def y_copy(chunk):
         return pltpu.make_async_remote_copy(
@@ -167,7 +187,7 @@
             def _():
                 z_copy(1, seq, chunk, me, src).start()
 
-    def spread(mine, chunk):
+    def token_spread(mine, chunk):
         seq = row if mine else 1 - row
 
         def turn(step, carry):
@@ -195,7 +215,7 @@
         ]
 
     def gain_columns(block):
-        return gains_ref.at[:, pl.ds(pl.multiple_of(block * width, width), width)]
+        return gains.at[:, pl.ds(pl.multiple_of(block * width, width), width)]
 
     def gain_copy(offset):
         return pltpu.make_async_remote_copy(
@@ -219,7 +239,7 @@
 
     def wo_region(owner, piece, side):
         start = pl.multiple_of(owner * lane_rows + piece * piece_rows, piece_rows)
-        return out_full_ref.at[
+        return out_full.at[
             pl.ds(start, piece_rows), pl.ds(pl.multiple_of(side * col_half, col_half), col_half)
         ]
 
@@ -280,7 +300,7 @@
 
     @pl.when(jnp.logical_not(home))
     def _():
-        for chunk in range(chunks):
+        for chunk in range(halves):
             y_copy(chunk).start()
 
     for piece in range(pieces):
@@ -308,11 +328,11 @@
 
     wo_local = pltpu.make_async_copy(
         wo_ref,
-        out_full_ref.at[:, pl.ds(pl.multiple_of(row * col_half, col_half), col_half)],
+        out_full.at[:, pl.ds(pl.multiple_of(row * col_half, col_half), col_half)],
         wo_sem,
     )
     loads = [
-        pltpu.make_async_copy(matrix, weights.at[index], w_sem.at[index])
+        pltpu.make_async_copy(matrix, qkv.at[pl.ds(index * half, half), :], w_sem.at[index])
         for index, matrix in enumerate((wq_ref, wk_ref, wv_ref))
     ]
     for load in loads:
@@ -343,7 +363,13 @@
     def build_bias(head, carry):
         tile = jnp.broadcast_to(lines[pl.ds(head, 1), :], (length, span))
         tile = pltpu.roll(tile, length + 1, 1, stride=1, stride_axis=0)
-        bias[head] = tile[:, :length]
+        for chunk in range(chunks):
+            bias[
+                chunk,
+                head // per_tile,
+                :,
+                pl.ds(pl.multiple_of(head % per_tile * length, length), length),
+            ] = tile[chunk * rows : (chunk + 1) * rows, :length]
         return carry
 
     lax.fori_loop(0, heads, build_bias, 0)
@@ -358,7 +384,7 @@
         return carry
 
     lax.fori_loop(1, count, gain_wait, 0)
-    gain_half = gains_ref[
+    gain_half = gains[
         pl.ds(0, 8), pl.ds(pl.multiple_of(row * half, half), half)
     ][0:1, :].astype(jnp.float32)
 
@@ -368,8 +394,8 @@
         return jnp.sum(values * values, axis=1, keepdims=True)
 
     def outgoing(chunk):
-        squares = multiply_gain(1 - row, chunk * rows, rows)
-        for start in range(0, rows, 128):
+        squares = multiply_gain(1 - row, chunk * half_rows, half_rows)
+        for start in range(0, half_rows, 128):
             sums_out[chunk, :, start : start + 128] = jnp.broadcast_to(
                 squares[start : start + 128], (128, 128)
             ).T[0:8]
@@ -379,8 +405,8 @@
             columns = pl.ds(pl.multiple_of(group * group_width, group_width), group_width)
             for index in range(3):
                 part_out[chunk, group, :, pl.ds(index * group_width, group_width)] = jnp.dot(
-                    scaled[pl.ds(chunk * rows, rows), :],
-                    weights[index, :, columns],
+                    scaled[pl.ds(chunk * half_rows, half_rows), :],
+                    qkv[pl.ds(index * half, half), columns],
                     preferred_element_type=jnp.float32,
                 ).astype(jnp.bfloat16)
             part_copy(chunk, group).start()
@@ -393,48 +419,54 @@
         for flip in (1, 2, 3):
             wo_fan(flip, piece, lane).start()
 
-    spread(True, 0)
+    token_spread(True, 0)
     launch(False, 0)
     fan(0)
-    spread(False, 0)
+    token_spread(False, 0)
     launch(False, 1)
     for load in loads:
         load.wait()
     fan(1)
     outgoing(0)
-    spread(False, 1)
+    token_spread(False, 1)
     launch(True, 1)
     fan(2)
     outgoing(1)
     fan(3)
-    spread(True, 1)
+    token_spread(True, 1)
     own_squares = multiply_gain(row, 0, length)
-    for chunk in range(chunks):
+    for chunk in range(halves):
         sum_copy(chunk).wait_recv()
     other_squares = jnp.concatenate(
         [
             jnp.broadcast_to(sums_in[chunk, 0:1, start : start + 128], (128, 128)).T[:, 0:1]
-            for chunk in range(chunks)
-            for start in range(0, rows, 128)
+            for chunk in range(halves)
+            for start in range(0, half_rows, 128)
         ]
     )
     scale = lax.rsqrt((own_squares + other_squares) / (count * width) + epsilon)
-    pair = 128 // head_size
+    members = 128 // head_size
     first_lanes = lax.broadcasted_iota(jnp.int32, (length, 128), 1)
 
-    def attend(group, carry):
-        columns = pl.ds(pl.multiple_of(group * group_width, group_width), group_width)
+    def bias_of(head):
+        lanes = pl.ds(pl.multiple_of(head % per_tile * length, length), length)
+        return jnp.concatenate(
+            [bias[chunk, head // per_tile, :, lanes] for chunk in range(chunks)]
+        )
+
+    def attend(member_group, carry):
+        columns = pl.ds(pl.multiple_of(member_group * group_width, group_width), group_width)
         products = [
-            jnp.dot(scaled[...], weights[index, :, columns], preferred_element_type=jnp.float32)
+            jnp.dot(scaled[...], qkv[pl.ds(index * half, half), columns], preferred_element_type=jnp.float32)
             for index in range(3)
         ]
-        for chunk in range(chunks):
-            part_copy(chunk, group).wait_recv()
+        for chunk in range(halves):
+            part_copy(chunk, member_group).wait_recv()
         query, key, value = [
             (
                 (
                     product
-                    + part_in[:, group, :, pl.ds(index * group_width, group_width)]
+                    + part_in[:, member_group, :, pl.ds(index * group_width, group_width)]
                     .astype(jnp.float32)
                     .reshape(length, group_width)
                 )
@@ -446,7 +478,7 @@
             cut = slice(tile * 128, (tile + 1) * 128)
             query_pair, key_pair, value_pair = query[:, cut], key[:, cut], value[:, cut]
             outcome = None
-            for member in range(pair):
+            for member in range(members):
                 mask = jnp.logical_and(
                     first_lanes >= member * head_size, first_lanes < (member + 1) * head_size
                 )
@@ -457,7 +489,7 @@
                         (((1,), (1,)), ((), ())),
                         preferred_element_type=jnp.float32,
                     )
-                    + bias[group * (group_width // head_size) + tile * pair + member]
+                    + bias_of(member_group * (group_width // head_size) + tile * members + member)
                 )
                 exponent = jnp.exp(scores - jnp.max(scores, axis=1, keepdims=True))
                 total = jnp.sum(exponent, axis=1, keepdims=True)
@@ -467,13 +499,20 @@
                     preferred_element_type=jnp.float32,
                 )
                 outcome = mixed if outcome is None else jnp.where(mask, mixed, outcome)
-            att_ref[
-                :, pl.ds(pl.multiple_of(group * group_width + tile * 128, 128), 128)
+            att[
+                :, pl.ds(pl.multiple_of(member_group * group_width + tile * 128, 128), 128)
             ] = outcome.astype(jnp.bfloat16)
         return carry
 
     lax.fori_loop(0, groups, attend, 0)
 
+    later = [
+        pltpu.make_async_copy(gate_ref, gate, d_sem.at[0]),
+        pltpu.make_async_copy(up_ref, up, d_sem.at[1]),
+        pltpu.make_async_copy(down_ref, down, d_sem.at[2]),
+    ]
+    later[0].start()
+    later[1].start()
     wo_local.wait()
     for piece in range(pieces):
         for flip in (1, 2, 3):
@@ -481,8 +520,8 @@
 
     def project(block, carry):
         columns = pl.ds(pl.multiple_of(block * width, width), width)
-        share_ref[block] = jnp.dot(
-            att_ref[...], out_full_ref[:, columns], preferred_element_type=jnp.float32
+        share[block] = jnp.dot(
+            att[...], out_full[:, columns], preferred_element_type=jnp.float32
         ).astype(jnp.bfloat16)
         return carry
 
@@ -491,158 +530,7 @@
         wo_y(piece).wait_send()
         for flip in (1, 2, 3):
             wo_fan(flip, piece, lane).wait_send()
-    for chunk in range(chunks):
-        sum_copy(chunk).wait_send()
-
-        def part_drain(group, carry):
-            part_copy(chunk, group).wait_send()
-            return carry
-
-        lax.fori_loop(0, groups, part_drain, 0)
-
-        @pl.when(jnp.logical_not(home))
-        def _():
-            y_copy(chunk).wait_send()
-
-        def z_drain(slot, carry):
-            block = slot + row * half_blocks
-            for seq in (0, 1):
-
-                @pl.when(jnp.logical_and(me < count - 1, block <= me))
-                def _():
-                    z_copy(0, seq, chunk, block).wait_send()
-
-                @pl.when(jnp.logical_and(me > 0, block >= me))
-                def _():
-                    z_copy(1, seq, chunk, block).wait_send()
-
-            return carry
-
-        lax.fori_loop(0, half_blocks, z_drain, 0)
-
-    def gain_drain(offset, carry):
-        gain_copy(offset).wait_send()
-        return carry
-
-    lax.fori_loop(1, count, gain_drain, 0)
-
-
-def front(tok, attn_gain, ffn_gain, table, wq, wk, wv, wo, count, collective_id):
-    length, width = tok.shape
-    chunks, pieces = 2, 4
-    inner = wq.shape[1]
-    heads = table.shape[1]
-    head_size = inner // heads
-    groups = max(1, inner // 256)
-    half = wq.shape[0]
-    rows = length // chunks
-    group_width = inner // groups
-    dma = pltpu.SemaphoreType.DMA
-    vmem = pl.BlockSpec(memory_space=pltpu.VMEM)
-    anywhere = pl.BlockSpec(memory_space=pl.ANY)
-    parts = pltpu.VMEM((chunks, groups, rows, 3 * group_width), jnp.bfloat16)
-    sums = pltpu.VMEM((chunks, 8, rows), jnp.float32)
-    return pl.pallas_call(
-        functools.partial(front_kernel, count, chunks, groups),
-        out_shape=(
-            jax.ShapeDtypeStruct((count, length, width), jnp.bfloat16),
-            jax.ShapeDtypeStruct((16, count * width), jnp.bfloat16),
-        ),
-        in_specs=[vmem] * 4 + [anywhere] * 4,
-        out_specs=(vmem, vmem),
-        scratch_shapes=[
-            pltpu.VMEM((length, inner), jnp.bfloat16),
-            pltpu.VMEM((wo.shape[0], 2 * wo.shape[1]), jnp.bfloat16),
-            pltpu.VMEM((2, length, half), jnp.bfloat16),
-            pltpu.VMEM((3, half, inner), jnp.bfloat16),
-            pltpu.VMEM((length, half), jnp.bfloat16),
-            parts,
-            parts,
-            sums,
-            sums,
-            pltpu.VMEM((heads, length, length), jnp.float32),
-            pltpu.VMEM((heads, 2 * length), jnp.float32),
-            pltpu.VMEM((16, width), jnp.bfloat16),
-            dma((3,)),
-            dma,
-            dma,
-            dma,
-            dma((count,)),
-            dma((count,)),
-            dma((chunks,)),
-            dma((chunks,)),
-            dma((2, 2, chunks, count // 2)),
-            dma((2, chunks, count // 2)),
-            dma((chunks, groups)),
-            dma((chunks, groups)),
-            dma((chunks,)),
-            dma((chunks,)),
-            dma((pieces,)),
-            dma((pieces,)),
-            dma((3, pieces)),
-            dma((3, pieces)),
-        ],
-        compiler_params=pltpu.CompilerParams(
-            collective_id=collective_id, has_side_effects=True, vmem_limit_bytes=56 * 2**20
-        ),
-    )(tok, attn_gain, ffn_gain, table, wq, wk, wv, wo)
-
-
-def back_kernel(
-    count,
-    chunks,
-    per,
-    spacing,
-    share_ref,
-    gains_ref,
-    tok_ref,
-    gate_ref,
-    up_ref,
-    down_ref,
-    out_ref,
-    gate,
-    up,
-    down,
-    group,
-    normed,
-    hidden,
-    pair,
-    kept,
-    total,
-    c_out,
-    c_in,
-    e_out,
-    e_in,
-    y_out,
-    y_in,
-    w_sem,
-    c_send,
-    c_recv,
-    e_send,
-    e_recv,
-    y_send,
-    y_recv,
-    z_send,
-    z_recv,
-    x_send,
-    x_recv,
-    r_send,
-    r_recv,
-):
-    me = lax.axis_index("ma")
-    row = lax.axis_index("row")
-    length, width = tok_ref.shape
-    rows = length // chunks
-    greet(me, count, row)
-
-    loads = [
-        pltpu.make_async_copy(source, target, w_sem.at[index])
-        for index, (source, target) in enumerate(
-            ((gate_ref, gate), (up_ref, up), (down_ref, down))
-        )
-    ]
-    for load in loads:
-        load.start()
+    later[2].start()
 
     def columns(block):
         return pl.ds(pl.multiple_of(block * width, width), width)
@@ -675,8 +563,8 @@
         return pltpu.make_async_remote_copy(
             src_ref=y_out.at[chunk, block],
             dst_ref=y_in.at[chunk, block],
-            send_sem=y_send.at[chunk, block],
-            recv_sem=y_recv.at[chunk, block],
+            send_sem=a_send.at[chunk, block],
+            recv_sem=a_recv.at[chunk, block],
             device_id={"row": 1 - row},
             device_id_type=MESH,
         )
@@ -689,8 +577,8 @@
         return pltpu.make_async_remote_copy(
             src_ref=here,
             dst_ref=here,
-            send_sem=z_send.at[way, chunk, block],
-            recv_sem=z_recv.at[chunk, block],
+            send_sem=d_send.at[way, chunk, block],
+            recv_sem=d_recv.at[chunk, block],
             device_id={"ma": me + 1 - 2 * way},
             device_id_type=MESH,
         )
@@ -754,7 +642,7 @@
         ).astype(jnp.bfloat16)
 
     attention_line = (c_out, c_in, c_send, c_recv)
-    hidden_line = (e_out, e_in, e_send, e_recv)
+    hidden_line = (c_out, e_in, e_send, e_recv)
 
     def chain(line, chunk, step, last):
         outs, ins, sends, recvs = line
@@ -770,7 +658,7 @@
                     across(chunk, block).wait_recv()
                     total[...] = kept[chunk, block] + y_in[chunk, block].astype(jnp.float32)
                 else:
-                    total[...] = share_ref[block, chunk_rows(chunk), :].astype(jnp.float32)
+                    total[...] = share[block, chunk_rows(chunk), :].astype(jnp.float32)
 
                 if rightward:
 
@@ -793,6 +681,8 @@
 
                     @pl.when(step > 0)
                     def _():
+                        if last:
+                            hop(*attention_line, chunk, block, True).wait_send()
                         outs[chunk, block] = total[...].astype(jnp.bfloat16)
                         hop(*line, chunk, block, True).start()
 
@@ -803,6 +693,8 @@
                         landed(*line, chunk, block, False).wait_recv()
                         total[...] = total[...] + ins[chunk, block].astype(jnp.float32)
 
+                    if last:
+                        hop(*attention_line, chunk, block, False).wait_send()
                     outs[chunk, block] = total[...].astype(jnp.bfloat16)
                     hop(*line, chunk, block, False).start()
 
@@ -865,7 +757,7 @@
             normed[pl.ds(pl.multiple_of(index * norm_rows, norm_rows), norm_rows), :] = (
                 values
                 * lax.rsqrt(mean_square + epsilon)
-                * gains_ref[8:9, :].astype(jnp.float32)
+                * gains[8:9, :].astype(jnp.float32)
             ).astype(jnp.bfloat16)
             return carry
 
@@ -873,7 +765,7 @@
 
         @pl.when(batch == 0)
         def _():
-            for load in loads:
+            for load in later:
                 load.wait()
 
         def gated(index, carry):
@@ -1001,12 +893,10 @@
 
         @pl.when(block > me)
         def _():
-            hop(*attention_line, chunk, block, True).wait_send()
             hop(*hidden_line, chunk, block, True).wait_send()
 
         @pl.when(block < me)
         def _():
-            hop(*attention_line, chunk, block, False).wait_send()
             hop(*hidden_line, chunk, block, False).wait_send()
 
         @pl.when(jnp.logical_and(me < count - 1, block <= me))
@@ -1022,38 +912,123 @@
     lax.fori_loop(0, chunks * count, drain, 0)
 
 
-def back(share, gains, tok, gate, up, down, count, chunks, collective_id):
+    for chunk in range(halves):
+        sum_copy(chunk).wait_send()
+
+        def part_drain(group, carry):
+            part_copy(chunk, group).wait_send()
+            return carry
+
+        lax.fori_loop(0, groups, part_drain, 0)
+
+        @pl.when(jnp.logical_not(home))
+        def _():
+            y_copy(chunk).wait_send()
+
+        def z_drain(slot, carry):
+            block = slot + row * half_blocks
+            for seq in (0, 1):
+
+                @pl.when(jnp.logical_and(me < count - 1, block <= me))
+                def _():
+                    z_copy(0, seq, chunk, block).wait_send()
+
+                @pl.when(jnp.logical_and(me > 0, block >= me))
+                def _():
+                    z_copy(1, seq, chunk, block).wait_send()
+
+            return carry
+
+        lax.fori_loop(0, half_blocks, z_drain, 0)
+
+    def gain_drain(offset, carry):
+        gain_copy(offset).wait_send()
+        return carry
+
+    lax.fori_loop(1, count, gain_drain, 0)
+
+
+def layer(
+    tok, attn_gain, ffn_gain, table, wq, wk, wv, wo, gate, up, down, count, collective_id
+):
     length, width = tok.shape
+    halves, chunks, per, spacing, pieces = 2, 4, 1, 2, 4
+    inner = wq.shape[1]
+    heads = table.shape[1]
+    groups = max(1, inner // 256)
+    half = wq.shape[0]
+    half_rows = length // halves
     rows = length // chunks
-    per, spacing = 1, 2
-    inner = down.shape[0]
+    group_width = inner // groups
+    per_tile = max(1, min(heads, width // length))
     dma = pltpu.SemaphoreType.DMA
     vmem = pl.BlockSpec(memory_space=pltpu.VMEM)
     anywhere = pl.BlockSpec(memory_space=pl.ANY)
-    line = pltpu.VMEM((chunks, count, rows, width), jnp.bfloat16)
-    longer = pltpu.VMEM((chunks, count + 1, rows, width), jnp.bfloat16)
+    bf16 = lambda *shape: pltpu.VMEM(shape, jnp.bfloat16)
+    f32 = lambda *shape: pltpu.VMEM(shape, jnp.float32)
+    bias_shape = (chunks, heads // per_tile, rows, per_tile * length)
+    kept_shape = (chunks, count, rows, width)
+    shared = bias_shape == kept_shape
+
+    def body(*refs):
+        refs = list(refs)
+        if shared:
+            refs.insert(31, refs[30])
+        layer_kernel(count, halves, groups, chunks, per, spacing, *refs)
+
     return pl.pallas_call(
-        functools.partial(back_kernel, count, chunks, per, spacing),
+        body,
         out_shape=jax.ShapeDtypeStruct((length, width), jnp.bfloat16),
-        in_specs=[vmem, vmem, vmem] + [anywhere] * 3,
+        in_specs=[vmem] * 4 + [anywhere] * 7,
         out_specs=vmem,
         scratch_shapes=[
-            pltpu.VMEM(gate.shape, jnp.bfloat16),
-            pltpu.VMEM(up.shape, jnp.bfloat16),
-            pltpu.VMEM(down.shape, jnp.bfloat16),
-            pltpu.VMEM((chunks, 2, rows, count * width), jnp.bfloat16),
-            pltpu.VMEM((2 * per * rows, count * width), jnp.bfloat16),
-            pltpu.VMEM((2 * per * rows, inner), jnp.bfloat16),
-            pltpu.VMEM((per, 2, rows, width), jnp.float32),
-            pltpu.VMEM((chunks, count, rows, width), jnp.float32),
-            pltpu.VMEM((rows, width), jnp.float32),
-            line,
-            longer,
-            line,
-            longer,
-            line,
-            line,
+            bf16(3 * half, inner),
+            bf16(*up.shape),
+            bf16(wo.shape[0], 2 * wo.shape[1]),
+            bf16(16, count * width),
+            bf16(2, length, half),
+            bf16(length, half),
+            bf16(halves, groups, half_rows, 3 * group_width),
+            bf16(halves, groups, half_rows, 3 * group_width),
+            f32(halves, 8, half_rows),
+            f32(halves, 8, half_rows),
+            f32(heads, 2 * length),
+            bf16(16, width),
+            bf16(length, inner),
+            bf16(count, length, width),
+            bf16(chunks, 2, rows, count * width),
+            bf16(2 * per * rows, count * width),
+            bf16(2 * per * rows, down.shape[0]),
+            f32(per, 2, rows, width),
+            f32(*bias_shape),
+        ]
+        + ([] if shared else [f32(*kept_shape)])
+        + [
+            f32(rows, width),
+            bf16(chunks, count, rows, width),
+            bf16(chunks, count + 1, rows, width),
+            bf16(chunks, count + 1, rows, width),
+            bf16(chunks, count, rows, width),
+            bf16(chunks, count, rows, width),
             dma((3,)),
+            dma((3,)),
+            dma,
+            dma,
+            dma,
+            dma((count,)),
+            dma((count,)),
+            dma((halves,)),
+            dma((halves,)),
+            dma((2, 2, halves, count // 2)),
+            dma((2, halves, count // 2)),
+            dma((halves, groups)),
+            dma((halves, groups)),
+            dma((halves,)),
+            dma((halves,)),
+            dma((pieces,)),
+            dma((pieces,)),
+            dma((3, pieces)),
+            dma((3, pieces)),
             dma((chunks, count)),
             dma((chunks, count + 1)),
             dma((chunks, count)),
@@ -1068,9 +1043,9 @@
             dma((2, chunks)),
         ],
         compiler_params=pltpu.CompilerParams(
-            collective_id=collective_id, has_side_effects=True, vmem_limit_bytes=60 * 2**20
+            collective_id=collective_id, has_side_effects=True, vmem_limit_bytes=67043328
         ),
-    )(share, gains, tok, gate, up, down)
+    )(tok, attn_gain, ffn_gain, table, wq, wk, wv, wo, gate, up, down)
 
 
 def on_device(
@@ -1090,7 +1065,7 @@
     ma_count = lax.axis_size("ma")
     slab_rows = sequences * length
     token_rows = tokens.reshape(slab_rows, part_width)
-    share, gains = front(
+    encoded = layer(
         token_rows,
         attn_gain,
         ffn_gain,
@@ -1099,18 +1074,10 @@
         key_weight,
         value_projection_matrix,
         attention_output_matrix,
-        ma_count,
-        3,
-    )
-    encoded = back(
-        share,
-        gains,
-        token_rows,
         gate_weight,
         up_weight,
         down_projection_weight,
         ma_count,
-        4,
         1,
     )
     return encoded.reshape(sequences, length, part_width)

time: 207 us -> 203 us (0.981)
  Pallas kernels: 203 us -> 199 us
    pallas_call x2 -> x1, Pallas kernels: 203 us -> 199 us  [layer(): pl.pallas_call(body, out_shape=jax.ShapeDtypeStruct((length, width), jnp....]
where the time goes in v4:
time: 203 us; the launch traced here: 202 us
  Pallas kernels  199 us (98%)
  local copies, waits for them, and re-layouts  3.24 us (2%)
    pallas_call x1, Pallas kernels, layer(): pl.pallas_call(body, out_shape=jax.ShapeDtypeStruct((length, width), jnp....  199 us

profile of v4, /device:TPU:0, one launch (start us, length us, event | category | flops | bytes accessed | tf_op | source)
XLA Modules:
  0.0 201.8 jit_solution(2959493284399536024)
XLA Ops:
  0.0 1.4 copy.12.refs_3_
  1.4 198.5 %shard_map.109 = bf16[256,1024]{1,0:T(8,128)(2,1)} custom-call(bf16[256,1024]{1,0:T(8,128)(2,1)} %bitcast.3, bf16[1024]{0:T(1024)(128)(2,1)} %refs_1_.1, bf16[1024]{0:T(1024)(128)(2,1)} %refs_2_.1, f32[32,16]{1,0:T(8,128)} %copy.12.refs_3_, bf16[2048,1024]{1,0:T(8,128)(2,1)} %refs_4_.1, bf16[2048,1024]{1,0:T(8,128)(2,1)} %refs_5_.1, ...), custom_call_target="tpu_custom_call" | custom-call | tf_op jit(solution)/shard_map/pallas_call | solution.py:979
  199.9 1.9 copy.14

commit v5 on v4

--- a/solution.py
+++ b/solution.py
@@ -102,7 +102,7 @@
     half_blocks = count // 2
     half = half_blocks * width
     inner = qkv.shape[1]
-    heads = table_ref.shape[1]
+    heads = table_ref.shape[0]
     head_size = inner // heads
     half_rows = length // halves
     group_width = inner // groups
@@ -350,12 +350,12 @@
         forward = forward + (distance >= threshold).astype(jnp.int32)
     bucket = jnp.where(offset > 0, forward, backward)
 
-    entries = lax.broadcasted_iota(jnp.int32, (table_ref.shape[0], span), 0)
+    entries = lax.broadcasted_iota(jnp.int32, (table_ref.shape[1], span), 0)
     chosen = (entries == jnp.broadcast_to(bucket[0:1, :], entries.shape)).astype(jnp.float32)
     lines[...] = lax.dot_general(
         table_ref[...],
         chosen,
-        (((0,), (0,)), ((), ())),
+        (((1,), (0,)), ((), ())),
         precision=lax.Precision.HIGHEST,
         preferred_element_type=jnp.float32,
     )
@@ -954,7 +954,7 @@
     length, width = tok.shape
     halves, chunks, per, spacing, pieces = 2, 4, 1, 2, 4
     inner = wq.shape[1]
-    heads = table.shape[1]
+    heads = table.shape[0]
     groups = max(1, inner // 256)
     half = wq.shape[0]
     half_rows = length // halves
@@ -1069,7 +1069,7 @@
         token_rows,
         attn_gain,
         ffn_gain,
-        bucket_bias_matrix,
+        bucket_bias_matrix.T,
         query_weight,
         key_weight,
         value_projection_matrix,

time: 203 us -> 202 us (level)
  no operation moved by 1% of the time
where the time goes in v5:
time: 202 us; the launch traced here: 200 us
  Pallas kernels  198 us (98%)
    pallas_call x1, Pallas kernels, layer(): pl.pallas_call(body, out_shape=jax.ShapeDtypeStruct((length, width), jnp....  198 us

profile of v5, /device:TPU:0, one launch (start us, length us, event | category | flops | bytes accessed | tf_op | source)
XLA Modules:
  0.0 200.1 jit_solution(16010754225568038537)
XLA Ops:
  0.0 198.3 %shard_map.109 = bf16[256,1024]{1,0:T(8,128)(2,1)} custom-call(bf16[256,1024]{1,0:T(8,128)(2,1)} %bitcast.4, bf16[1024]{0:T(1024)(128)(2,1)} %refs_1_.1, bf16[1024]{0:T(1024)(128)(2,1)} %refs_2_.1, f32[16,32]{1,0:T(8,128)} %bitcast.5, bf16[2048,1024]{1,0:T(8,128)(2,1)} %refs_4_.1, bf16[2048,1024]{1,0:T(8,128)(2,1)} %refs_5_.1, bf16[2048,1024]{1,0:T(8,128)(2,1)} %refs_6_.1, ...), custom_call_target="tpu_custom_call" | custom-call | tf_op jit(solution)/shard_map/pallas_call | solution.py:979
  198.3 1.9 copy.13
